TPU v7x, 32 devices: a whole 2x2x4 slice. The times are simulated.
32 devices in a mesh: data: 4 (over x, y), seq: 8 (over z, core).
Axes of the slice: x: 2, y: 2, z: 4, core: 2. Of those that a mesh axis runs over, the one named last changes fastest.
Arguments:
- x_in: bfloat16 [3, 4096, 4096], P(None, ('data', 'seq')), parts along dimension 1
- positions: int32 [4096], P(('data', 'seq')), parts along dimension 0
- w_query: bfloat16 [3, 4096, 32, 128], replicated
- w_key: bfloat16 [3, 4096, 32, 128], replicated
- w_value: bfloat16 [3, 4096, 32, 128], replicated
- w_out: bfloat16 [3, 32, 128, 4096], replicated
- w_up: bfloat16 [3, 4096, 11008], replicated
- w_down: bfloat16 [3, 11008, 4096], replicated
- g_attn: float32 [3, 4096], replicated
- g_mlp: float32 [3, 4096], replicated
Outputs:
- output: bfloat16 [3, 4096, 4096], P(None, ('data', 'seq')), parts along dimension 1
There are 4 independent parts. A program takes and returns all parts, laid end to end along the dimension named above; an argument that names none is the same for every part.
All inputs are finite; a program needn't handle non-finite values.
Results may differ from a plain program's by a relative error of at most 0.0164023.
Values are sent between devices in bfloat16 or wider.
A program may use at most 3.75 GiB of HBM per device.

v0:
```python
import jax
import jax.numpy as jnp
from jax import lax
from jax.sharding import PartitionSpec as P

ROPE_BASE = 10000.0
NORM_EPS = 1e-6


def rms_norm(x_act, gain_vec):
    x_f32 = x_act.astype(jnp.float32)
    mean_sq = jnp.mean(x_f32 * x_f32, axis=-1, keepdims=True)
    return (x_f32 * lax.rsqrt(mean_sq + NORM_EPS) * gain_vec).astype(jnp.bfloat16)


def rope_tables(positions, head_dim):
    inv_freq = ROPE_BASE ** (-jnp.arange(head_dim // 2, dtype=jnp.float32) * (2.0 / head_dim))
    angles = positions.astype(jnp.float32)[..., None] * inv_freq
    return jnp.cos(angles), jnp.sin(angles)


def apply_rope(proj_f32, cos_t, sin_t):
    half_dim = proj_f32.shape[-1] // 2
    x_first = proj_f32[..., :half_dim]
    x_second = proj_f32[..., half_dim:]
    cos_b = cos_t[..., None, :]
    sin_b = sin_t[..., None, :]
    return jnp.concatenate([x_first * cos_b - x_second * sin_b, x_second * cos_b + x_first * sin_b], axis=-1).astype(jnp.bfloat16)


def causal_attention(q_heads, k_heads, v_heads, q_offset, q_block):
    n_batch, q_len, kv_heads, groups, head_dim = q_heads.shape
    key_len = k_heads.shape[1]
    n_blocks = q_len // q_block
    att_scale = head_dim ** -0.5
    key_pos = jnp.arange(key_len)

    def one_block(blk_idx):
        blk_start = blk_idx * q_block
        q_blk = lax.dynamic_slice_in_dim(q_heads, blk_start, q_block, axis=1)
        scores = jnp.einsum("bqkgd,bskd->bkgqs", q_blk, k_heads, preferred_element_type=jnp.float32) * att_scale
        query_pos = q_offset + blk_start + jnp.arange(q_block)
        scores = jnp.where(key_pos[None, :] <= query_pos[:, None], scores, -1e30)
        row_max = jnp.max(scores, axis=-1, keepdims=True)
        exp_f32 = jnp.exp(scores - row_max)
        row_sum = jnp.sum(exp_f32, axis=-1)
        weighted = jnp.einsum("bkgqs,bskd->bqkgd", exp_f32.astype(jnp.bfloat16), v_heads, preferred_element_type=jnp.float32)
        return (weighted / jnp.transpose(row_sum, (0, 3, 1, 2))[..., None]).astype(jnp.bfloat16)

    blocks = lax.map(one_block, jnp.arange(n_blocks))
    return jnp.moveaxis(blocks, 0, 1).reshape(n_batch, q_len, kv_heads * groups, head_dim)


def layer_step(hidden, cos_t, sin_t, w_query, w_key, w_value, w_out, w_up, w_down, gain_attn, gain_mlp):
    normed = rms_norm(hidden, gain_attn)
    q_loc = apply_rope(jnp.einsum("bsd,dhe->bshe", normed, w_query, preferred_element_type=jnp.float32), cos_t, sin_t)
    k_loc = apply_rope(jnp.einsum("bsd,dhe->bshe", normed, w_key, preferred_element_type=jnp.float32), cos_t, sin_t)
    v_loc = jnp.einsum("bsd,dhe->bshe", normed, w_value, preferred_element_type=jnp.float32).astype(jnp.bfloat16)
    q_all = lax.all_to_all(q_loc, "seq", 2, 1, tiled=True)
    k_all = lax.all_to_all(k_loc, "seq", 2, 1, tiled=True)
    v_all = lax.all_to_all(v_loc, "seq", 2, 1, tiled=True)
    n_batch, seq_len, heads_loc, head_dim = q_all.shape
    kv_loc = k_all.shape[2]
    q_grouped = q_all.reshape(n_batch, seq_len, kv_loc, heads_loc // kv_loc, head_dim)
    attn_heads = causal_attention(q_grouped, k_all, v_all, 0, min(256, seq_len))
    attn_loc = lax.all_to_all(attn_heads, "seq", 1, 2, tiled=True)
    resid_h = (hidden.astype(jnp.float32) + jnp.einsum("bshe,hed->bsd", attn_loc, w_out, preferred_element_type=jnp.float32)).astype(jnp.bfloat16)
    normed_mlp = rms_norm(resid_h, gain_mlp)
    gelu_act = jax.nn.gelu(jnp.einsum("bsd,df->bsf", normed_mlp, w_up, preferred_element_type=jnp.float32), approximate=True).astype(jnp.bfloat16)
    layer_out = resid_h.astype(jnp.float32) + jnp.einsum("bsf,fd->bsd", gelu_act, w_down, preferred_element_type=jnp.float32)
    return layer_out.astype(jnp.bfloat16)


def solution(mesh):
    tok_spec = P(None, ("data", "seq"), None)
    in_specs = (tok_spec, P(("data", "seq"))) + (P(),) * 8

    def device_fn(x_loc, pos_loc, w_query, w_key, w_value, w_out, w_up, w_down, g_attn, g_mlp):
        cos_t, sin_t = rope_tables(pos_loc, w_query.shape[-1])
        hidden = x_loc
        for layer_idx in range(w_query.shape[0]):
            hidden = layer_step(hidden, cos_t, sin_t, w_query[layer_idx], w_key[layer_idx], w_value[layer_idx], w_out[layer_idx], w_up[layer_idx], w_down[layer_idx], g_attn[layer_idx], g_mlp[layer_idx])
        return hidden

    return jax.shard_map(device_fn, mesh=mesh, in_specs=in_specs, out_specs=tok_spec, check_vma=False)
```

profile of v0, /device:TPU:0, one launch (start us, length us, event | category | flops | bytes accessed | tf_op | source)
XLA Modules:
  0.0 1821.1 jit_solution(13597462595924853674)
XLA Ops:
  2.2 64.9 %fusion.259 = (bf16[1,4096,32,128]{3,2,1,0:T(8,128)(2,1)}, bf16[1,4096,32,128]{3,2,1,0:T(8,128)(2,1)}, bf16[1,4096,32,128]{3,2,1,0:T(8,128)(2,1)}) fusion(bf16[3,4096,32,128]{3,2,1,0:T(8,128)(2,1)} %param.19), kind=kLoop, calls=%fused_computation.250 | loop fusion | bytes 201326592 | tf_op jit(solution)/shard_map/slice | solution.py:82
  67.1 43.0 %copy.105 = bf16[1,4096,32,128]{1,3,2,0:T(8,128)(2,1)} copy(bf16[1,4096,32,128]{3,2,1,0:T(8,128)(2,1)} %get-tuple-element.208) | data formatting | bytes 67108864
  110.8 64.7 %fusion.260 = (bf16[1,4096,32,128]{3,2,1,0:T(8,128)(2,1)}, bf16[1,4096,32,128]{3,2,1,0:T(8,128)(2,1)}, bf16[1,4096,32,128]{3,2,1,0:T(8,128)(2,1)}) fusion(bf16[3,4096,32,128]{3,2,1,0:T(8,128)(2,1)} %param.18), kind=kLoop, calls=%fused_computation.251 | loop fusion | bytes 201326592 | tf_op jit(solution)/shard_map/slice | solution.py:82
  175.4 42.7 %copy.104 = bf16[1,4096,32,128]{1,3,2,0:T(8,128)(2,1)} copy(bf16[1,4096,32,128]{3,2,1,0:T(8,128)(2,1)} %get-tuple-element.211) | data formatting | bytes 67108864
  218.1 21.8 %fusion.116 = f32[3,128,32,128]{1,3,2,0:T(8,128)S(1)} fusion(bf16[1,4096,32,128]{1,3,2,0:T(8,128)(2,1)} %copy.105, bf16[3,128,4096]{2,1,0:T(8,128)(2,1)S(1)} %copy-done.4, f32[4096]{0:T(1024)S(1)} %bitcast.520, f32[3,128]{1,0:T(4,128)S(1)} %add_rsqrt_fusion.5), kind=kOutput, calls=%fused_computation.110 | convolution fusion | flops 12891193344 | bytes 43009536 | tf_op jit(solution)/shard_map/bsd,dhe->bshe/dot_general | solution.py:57
  239.9 21.8 %fusion.118 = f32[3,128,32,128]{1,3,2,0:T(8,128)S(1)} fusion(bf16[1,4096,32,128]{1,3,2,0:T(8,128)(2,1)} %copy.104, bf16[3,128,4096]{2,1,0:T(8,128)(2,1)S(1)} %copy-done.4, f32[4096]{0:T(1024)S(1)} %bitcast.521, f32[3,128]{1,0:T(4,128)S(1)} %add_rsqrt_fusion.5), kind=kOutput, calls=%fused_computation.112 | convolution fusion | flops 12891193344 | bytes 43009536 | tf_op jit(solution)/shard_map/bsd,dhe->bshe/dot_general | solution.py:56
  267.4 16.6 all-to-all-start.1
  288.3 67.0 %all-to-all-done.1 = bf16[3,128,32,128]{1,3,0,2:T(8,128)(2,1)S(1)} async-done(((bf16[3,128,32,128]{1,3,0,2:T(8,128)(2,1)}), bf16[3,128,32,128]{1,3,0,2:T(8,128)(2,1)S(1)}, u32[]{:S(2)}, u32[]{:S(2)}) %all-to-all-start.1) | async-done | bytes 3145760 | tf_op jit(solution)/shard_map/all_to_all | solution.py:60
  359.8 64.8 %fusion.258 = (bf16[1,4096,32,128]{3,2,1,0:T(8,128)(2,1)}, bf16[1,4096,32,128]{3,2,1,0:T(8,128)(2,1)}, bf16[1,4096,32,128]{3,2,1,0:T(8,128)(2,1)}) fusion(bf16[3,4096,32,128]{3,2,1,0:T(8,128)(2,1)} %param.20), kind=kLoop, calls=%fused_computation.249 | loop fusion | bytes 201326592 | tf_op jit(solution)/shard_map/slice | solution.py:82
  424.6 18.1 fusion.234
  457.7 63.1 %all-to-all-done.2 = bf16[3,128,32,128]{3,1,0,2:T(8,128)(2,1)} async-done(((bf16[3,128,32,128]{3,1,0,2:T(8,128)(2,1)}), bf16[3,128,32,128]{3,1,0,2:T(8,128)(2,1)}, u32[]{:S(2)}, u32[]{:S(2)}) %all-to-all-start.2) | async-done | bytes 3145760 | tf_op jit(solution)/shard_map/all_to_all | solution.py:61
  527.2 55.9 %while.33 = (s32[]{:T(128)}, bf16[4,3,256,4,1,128]{5,2,0,3,1,4:T(8,128)(2,1)}, s32[4]{0:T(128)S(1)}, bf16[3,1024,4,1,128]{4,1,2,0,3:T(8,128)(2,1)}, bf16[3,1024,...) while((s32[]{:T(128)}, ...), condition=%wide.region_4.5_spmd.clone, body=%wide.region_1.4_spmd.clone.sunk | while | flops 1646258432 | bytes 59308736 | solution.py:50
  535.9 5.3 fusion.333
  549.9 5.3 fusion.333
  583.2 5.9 copy.63
  593.2 42.7 %copy.107 = bf16[1,4096,32,128]{1,3,2,0:T(8,128)(2,1)} copy(bf16[1,4096,32,128]{3,2,1,0:T(8,128)(2,1)} %get-tuple-element.210) | data formatting | bytes 67108864
  635.9 42.8 %copy.108 = bf16[1,4096,32,128]{1,3,2,0:T(8,128)(2,1)} copy(bf16[1,4096,32,128]{3,2,1,0:T(8,128)(2,1)} %get-tuple-element.207) | data formatting | bytes 67108864
  681.2 18.0 fusion.175
  700.9 49.2 %fusion.130.clone.3.clone.5 = bf16[3,128,11008]{2,1,0:T(8,128)(2,1)} fusion(bf16[3,4096,11008]{2,1,0:T(8,128)(2,1)} %param.22, bf16[3,128,4096]{2,1,0:T(8,128)(2,1)S(1)} %get-tuple-element.239, f32[4096]{0:T(1024)S(1)} %bitcast.523, f32[3,128]{1,0:T(4,128)S(1)} %add_rsqrt_fusion.4), kind=kOutput, calls=%fused_computation.127.clone.clone.clone.clone.clone.clone.clone.2 | convolution fusion | flops 34672508928 | bytes 101795328 | tf_op jit(solution)/shard_map/bsd,df->bsf/dot_general | solution.py:69
  750.1 43.7 %fusion.179 = (f32[3,128]{1,0:T(4,128)S(1)}, bf16[3,128,4096]{2,1,0:T(8,128)(2,1)S(1)}) fusion(bf16[3,11008,4096]{2,1,0:T(8,128)(2,1)} %param.23, bf16[3,128,4096]{2,1,0:T(8,128)(2,1)} %copy-done.28, bf16[3,128,11008]{2,1,0:T(8,128)(2,1)} %fusion.130.clone.3.clone.5), kind=kOutput, calls=%fused_computation.182 | convolution fusion | flops 34637611008 | bytes 104924672 | tf_op jit(solution)/shard_map/bsf,fd->bsd/dot_general | solution.py:70
  793.8 19.1 %fusion.235 = bf16[3,128,32,128]{3,1,2,0:T(8,128)(2,1)S(1)} fusion(bf16[1,4096,32,128]{3,2,1,0:T(8,128)(2,1)} %get-tuple-element.204, bf16[3,128,4096]{2,1,0:T(8,128)(2,1)S(1)} %get-tuple-element.241, f32[4096]{0:T(1024)S(1)} %bitcast.516, f32[3,128]{1,0:T(4,128)S(1)} %add_rsqrt_fusion.3), kind=kOutput, calls=%fused_computation.226 | convolution fusion | flops 12892766208 | bytes 39863808 | tf_op jit(solution)/shard_map/bsd,dhe->bshe/dot_general | solution.py:58
  819.9 22.9 %fusion.112 = f32[3,128,32,128]{1,3,2,0:T(8,128)S(1)} fusion(bf16[1,4096,32,128]{1,3,2,0:T(8,128)(2,1)} %copy.107, bf16[3,128,4096]{2,1,0:T(8,128)(2,1)} %copy-done.21, f32[4096]{0:T(1024)S(1)} %bitcast.517, f32[3,128]{1,0:T(4,128)S(1)} %add_rsqrt_fusion.3), kind=kOutput, calls=%fused_computation.106 | convolution fusion | flops 12891193344 | bytes 43009536 | tf_op jit(solution)/shard_map/bsd,dhe->bshe/dot_general | solution.py:56
  842.8 21.8 %fusion.110 = f32[3,128,32,128]{1,3,2,0:T(8,128)S(1)} fusion(bf16[1,4096,32,128]{1,3,2,0:T(8,128)(2,1)} %copy.108, bf16[3,128,4096]{2,1,0:T(8,128)(2,1)S(1)} %copy-done.22, f32[4096]{0:T(1024)S(1)} %bitcast.518, f32[3,128]{1,0:T(4,128)S(1)} %add_rsqrt_fusion.3), kind=kOutput, calls=%fused_computation.104 | convolution fusion | flops 12891193344 | bytes 43009536 | tf_op jit(solution)/shard_map/bsd,dhe->bshe/dot_general | solution.py:57
  870.1 21.2 %all-to-all-done.6 = bf16[3,128,32,128]{3,1,0,2:T(8,128)(2,1)S(1)} async-done(((bf16[3,128,32,128]{3,1,0,2:T(8,128)(2,1)}), bf16[3,128,32,128]{3,1,0,2:T(8,128)(2,1)S(1)}, u32[]{:S(2)}, u32[]{:S(2)}) %all-to-all-start.6) | async-done | bytes 3145760 | tf_op jit(solution)/shard_map/all_to_all | solution.py:61
  900.0 66.9 %all-to-all-done.5 = bf16[3,128,32,128]{1,3,0,2:T(8,128)(2,1)} async-done(((bf16[3,128,32,128]{1,3,0,2:T(8,128)(2,1)}), bf16[3,128,32,128]{1,3,0,2:T(8,128)(2,1)}, u32[]{:S(2)}, u32[]{:S(2)}) %all-to-all-start.5) | async-done | bytes 3145760 | tf_op jit(solution)/shard_map/all_to_all | solution.py:60
  976.9 65.9 %all-to-all-done.4 = bf16[3,128,32,128]{1,3,0,2:T(8,128)(2,1)} async-done(((bf16[3,128,32,128]{1,3,0,2:T(8,128)(2,1)}), bf16[3,128,32,128]{1,3,0,2:T(8,128)(2,1)}, u32[]{:S(2)}, u32[]{:S(2)}) %all-to-all-start.4) | async-done | bytes 3145760 | tf_op jit(solution)/shard_map/all_to_all | solution.py:59
  1049.9 56.0 %while.34 = (s32[]{:T(128)}, bf16[4,3,256,4,1,128]{5,2,0,3,1,4:T(8,128)(2,1)}, s32[4]{0:T(128)S(1)}, bf16[3,1024,4,1,128]{4,1,2,0,3:T(8,128)(2,1)}, bf16[3,1024,...) while((s32[]{:T(128)}, ...), condition=%wide.region_10.11_spmd.clone, body=%wide.region_7.10_spmd.clone.sunk | while | flops 1646258432 | bytes 59308736 | solution.py:50
  1086.5 5.3 fusion.339
  1105.8 5.9 copy.76
  1115.8 42.7 %copy.110 = bf16[1,4096,32,128]{1,3,2,0:T(8,128)(2,1)} copy(bf16[1,4096,32,128]{3,2,1,0:T(8,128)(2,1)} %get-tuple-element.209) | data formatting | bytes 67108864
  1158.6 42.7 %copy.111 = bf16[1,4096,32,128]{1,3,2,0:T(8,128)(2,1)} copy(bf16[1,4096,32,128]{3,2,1,0:T(8,128)(2,1)} %get-tuple-element.206) | data formatting | bytes 67108864
  1203.2 18.0 fusion.183
  1222.8 49.1 %fusion.138.clone.3.clone.5 = bf16[3,128,11008]{2,1,0:T(8,128)(2,1)} fusion(bf16[3,4096,11008]{2,1,0:T(8,128)(2,1)} %param.22, bf16[3,128,4096]{2,1,0:T(8,128)(2,1)S(1)} %get-tuple-element.243, f32[4096]{0:T(1024)S(1)} %bitcast.519, f32[3,128]{1,0:T(4,128)S(1)} %add_rsqrt_fusion.2), kind=kOutput, calls=%fused_computation.135.clone.clone.clone.clone.clone.clone.clone.2 | convolution fusion | flops 34672508928 | bytes 101795328 | tf_op jit(solution)/shard_map/bsd,df->bsf/dot_general | solution.py:69
  1271.9 43.7 %fusion.187 = (f32[3,128]{1,0:T(4,128)S(1)}, bf16[3,128,4096]{2,1,0:T(8,128)(2,1)S(1)}) fusion(bf16[3,11008,4096]{2,1,0:T(8,128)(2,1)} %param.23, bf16[3,128,4096]{2,1,0:T(8,128)(2,1)} %copy-done.27, bf16[3,128,11008]{2,1,0:T(8,128)(2,1)} %fusion.138.clone.3.clone.5), kind=kOutput, calls=%fused_computation.190 | convolution fusion | flops 34637611008 | bytes 104924672 | tf_op jit(solution)/shard_map/bsf,fd->bsd/dot_general | solution.py:70
  1315.6 19.1 %fusion.236 = bf16[3,128,32,128]{3,1,2,0:T(8,128)(2,1)S(1)} fusion(bf16[1,4096,32,128]{3,2,1,0:T(8,128)(2,1)} %get-tuple-element.203, bf16[3,128,4096]{2,1,0:T(8,128)(2,1)S(1)} %get-tuple-element.245, f32[4096]{0:T(1024)S(1)} %bitcast.512, f32[3,128]{1,0:T(4,128)S(1)} %add_rsqrt_fusion.1), kind=kOutput, calls=%fused_computation.227 | convolution fusion | flops 12892766208 | bytes 39863808 | tf_op jit(solution)/shard_map/bsd,dhe->bshe/dot_general | solution.py:58
  1341.8 22.9 %fusion.106 = f32[3,128,32,128]{1,3,2,0:T(8,128)S(1)} fusion(bf16[1,4096,32,128]{1,3,2,0:T(8,128)(2,1)} %copy.110, bf16[3,128,4096]{2,1,0:T(8,128)(2,1)} %copy-done.24, f32[4096]{0:T(1024)S(1)} %bitcast.513, f32[3,128]{1,0:T(4,128)S(1)} %add_rsqrt_fusion.1), kind=kOutput, calls=%fused_computation.100 | convolution fusion | flops 12891193344 | bytes 43009536 | tf_op jit(solution)/shard_map/bsd,dhe->bshe/dot_general | solution.py:56
  1364.6 21.8 %fusion.104 = f32[3,128,32,128]{1,3,2,0:T(8,128)S(1)} fusion(bf16[1,4096,32,128]{1,3,2,0:T(8,128)(2,1)} %copy.111, bf16[3,128,4096]{2,1,0:T(8,128)(2,1)S(1)} %copy-done.25, f32[4096]{0:T(1024)S(1)} %bitcast.514, f32[3,128]{1,0:T(4,128)S(1)} %add_rsqrt_fusion.1), kind=kOutput, calls=%fused_computation.98 | convolution fusion | flops 12891193344 | bytes 43009536 | tf_op jit(solution)/shard_map/bsd,dhe->bshe/dot_general | solution.py:57
  1391.9 21.1 %all-to-all-done.10 = bf16[3,128,32,128]{3,1,0,2:T(8,128)(2,1)S(1)} async-done(((bf16[3,128,32,128]{3,1,0,2:T(8,128)(2,1)}), bf16[3,128,32,128]{3,1,0,2:T(8,128)(2,1)S(1)}, u32[]{:S(2)}, u32[]{:S(2)}) %all-to-all-start.10) | async-done | bytes 3145760 | tf_op jit(solution)/shard_map/all_to_all | solution.py:61
  1421.8 66.9 %all-to-all-done.9 = bf16[3,128,32,128]{1,3,0,2:T(8,128)(2,1)} async-done(((bf16[3,128,32,128]{1,3,0,2:T(8,128)(2,1)}), bf16[3,128,32,128]{1,3,0,2:T(8,128)(2,1)}, u32[]{:S(2)}, u32[]{:S(2)}) %all-to-all-start.9) | async-done | bytes 3145760 | tf_op jit(solution)/shard_map/all_to_all | solution.py:60
  1498.8 65.8 %all-to-all-done.8 = bf16[3,128,32,128]{1,3,0,2:T(8,128)(2,1)} async-done(((bf16[3,128,32,128]{1,3,0,2:T(8,128)(2,1)}), bf16[3,128,32,128]{1,3,0,2:T(8,128)(2,1)}, u32[]{:S(2)}, u32[]{:S(2)}) %all-to-all-start.8) | async-done | bytes 3145760 | tf_op jit(solution)/shard_map/all_to_all | solution.py:59
  1571.7 56.2 %while.35 = (s32[]{:T(128)}, bf16[4,3,256,4,1,128]{5,2,0,3,1,4:T(8,128)(2,1)}, s32[4]{0:T(128)S(1)}, bf16[3,1024,4,1,128]{4,1,2,0,3:T(8,128)(2,1)}, bf16[3,1024,...) while((s32[]{:T(128)}, ...), condition=%wide.region_16.17_spmd.clone, body=%wide.region_13.16_spmd.clone.sunk | while | flops 1646258432 | bytes 59308736 | solution.py:50
  1580.5 5.3 fusion.345
  1608.6 5.3 fusion.345
  1622.7 5.3 fusion.345
  1632.3 75.7 %all_to_all.207 = bf16[3,1024,4,128]{3,2,0,1:T(4,128)(2,1)S(1)} all-to-all(bf16[3,1024,4,128]{3,2,0,1:T(4,128)(2,1)S(1)} %copy.89), channel_id=1, replica_groups=mesh['data'=4,'seq'=8] {'seq'}, dimensions={1} | all-to-all | bytes 6291456 | tf_op jit(solution)/shard_map/all_to_all | solution.py:66
  1709.8 18.0 fusion.191
  1727.9 49.2 %fusion.146.clone.7 = bf16[3,128,11008]{2,1,0:T(8,128)(2,1)} fusion(bf16[3,4096,11008]{2,1,0:T(8,128)(2,1)} %param.22, bf16[3,128,4096]{2,1,0:T(8,128)(2,1)S(1)} %get-tuple-element.247, f32[4096]{0:T(1024)S(1)} %bitcast.515, f32[3,128]{1,0:T(4,128)S(1)} %add_rsqrt_fusion), kind=kOutput, calls=%fused_computation.143.clone.clone.clone.clone.clone.2 | convolution fusion | flops 34672508928 | bytes 101795328 | tf_op jit(solution)/shard_map/bsd,df->bsf/dot_general | solution.py:69
  1777.0 43.6 %fusion.194 = bf16[3,128,4096]{2,1,0:T(8,128)(2,1)} fusion(bf16[3,128,4096]{2,1,0:T(8,128)(2,1)S(1)} %get-tuple-element.247, bf16[3,11008,4096]{2,1,0:T(8,128)(2,1)} %param.23, bf16[3,128,11008]{2,1,0:T(8,128)(2,1)} %fusion.146.clone.7), kind=kOutput, calls=%fused_computation.197 | convolution fusion | flops 34632892416 | bytes 104923136 | tf_op jit(solution)/shard_map/bsf,fd->bsd/dot_general | solution.py:70
  (207 shorter events, 265.2 us)
Async XLA Ops:
  67.1 43.0 %copy-start.4 = (bf16[3,128,4096]{2,1,0:T(8,128)(2,1)S(1)}, bf16[3,128,4096]{2,1,0:T(8,128)(2,1)}, u32[]{:S(2)}) copy-start(bf16[3,128,4096]{2,1,0:T(8,128)(2,1)} %param.16) | copy-start | bytes 9437188
  175.4 42.7 %copy-start.18 = (f32[1,4096]{1,0:T(1,128)S(1)}, f32[1,4096]{1,0:T(1,128)}, u32[]{:S(2)}) copy-start(f32[1,4096]{1,0:T(1,128)} %get-tuple-element.230) | copy-start | bytes 49156
  239.9 21.8 %copy-start.20 = (s32[128]{0:T(128)S(1)}, s32[128]{0:T(128)}, u32[]{:S(2)}) copy-start(s32[128]{0:T(128)} %param.17) | copy-start | bytes 1540
  239.9 21.8 %copy-start.19 = (f32[64]{0:T(128)S(1)}, f32[64]{0:T(128)}, u32[]{:S(2)}) copy-start(f32[64]{0:T(128)} %multiply_power_fusion) | copy-start | bytes 772
  262.0 3.1 copy-start.7
  262.0 3.1 copy-start.10
  267.4 87.9 %all-to-all-start.1 = ((bf16[3,128,32,128]{1,3,0,2:T(8,128)(2,1)}), bf16[3,128,32,128]{1,3,0,2:T(8,128)(2,1)S(1)}, u32[]{:S(2)}, u32[]{:S(2)}) async-start(bf16[3,128,32,128]{1,3,0,2:T(8,128)(2,1)} %copy.57), calls=%async_computation.1 | async-start | bytes 6291456 | tf_op jit(solution)/shard_map/all_to_all | solution.py:60
  355.3 69.2 %copy-start = (bf16[3,128,32,128]{1,3,0,2:T(8,128)(2,1)}, bf16[3,128,32,128]{1,3,0,2:T(8,128)(2,1)S(1)}, u32[]{:S(2)}) copy-start(bf16[3,128,32,128]{1,3,0,2:T(8,128)(2,1)S(1)} %all-to-all-done.1) | copy-start | bytes 9437188
  355.3 89.2 %all-to-all-start = ((bf16[3,128,32,128]{1,3,0,2:T(8,128)(2,1)}), bf16[3,128,32,128]{1,3,0,2:T(8,128)(2,1)}, u32[]{:S(2)}, u32[]{:S(2)}) async-start(bf16[3,128,32,128]{1,3,0,2:T(8,128)(2,1)} %copy.54), calls=%async_computation | async-start | bytes 6291456 | tf_op jit(solution)/shard_map/all_to_all | solution.py:59
  359.8 64.8 %copy-start.5 = (bf16[3,128,4096]{2,1,0:T(8,128)(2,1)S(1)}, bf16[3,128,4096]{2,1,0:T(8,128)(2,1)}, u32[]{:S(2)}) copy-start(bf16[3,128,4096]{2,1,0:T(8,128)(2,1)} %param.16) | copy-start | bytes 9437188
  444.5 76.3 %all-to-all-start.2 = ((bf16[3,128,32,128]{3,1,0,2:T(8,128)(2,1)}), bf16[3,128,32,128]{3,1,0,2:T(8,128)(2,1)}, u32[]{:S(2)}, u32[]{:S(2)}) async-start(bf16[3,128,32,128]{3,1,0,2:T(8,128)(2,1)} %copy.60), calls=%async_computation.2 | async-start | bytes 6291456 | tf_op jit(solution)/shard_map/all_to_all | solution.py:61
  532.2 3.7 copy-start.3
  546.2 3.7 copy-start.3
  560.2 3.7 copy-start.3
  574.1 3.7 copy-start.3
  589.1 90.2 %all-to-all-start.3 = ((bf16[3,1024,4,128]{3,2,0,1:T(4,128)(2,1)}), bf16[3,1024,4,128]{3,2,0,1:T(4,128)(2,1)S(1)}, u32[]{:S(2)}, u32[]{:S(2)}) async-start(bf16[3,1024,4,128]{3,2,0,1:T(4,128)(2,1)} %copy.63), calls=%async_computation.3 | async-start | bytes 6291456 | tf_op jit(solution)/shard_map/all_to_all | solution.py:66
  635.9 42.8 %copy-start.13 = (f32[3,4096]{1,0:T(4,128)S(1)}, f32[3,4096]{1,0:T(4,128)}, u32[]{:S(2)}) copy-start(f32[3,4096]{1,0:T(4,128)} %param.25) | copy-start | bytes 147460
  679.3 1.9 copy-start.6
  699.2 1.7 copy-start.28
  750.1 43.7 %copy-start.16 = (f32[1,4096]{1,0:T(1,128)S(1)}, f32[1,4096]{1,0:T(1,128)}, u32[]{:S(2)}) copy-start(f32[1,4096]{1,0:T(1,128)} %get-tuple-element.231) | copy-start | bytes 49156
  793.8 19.2 %copy-start.21 = (bf16[3,128,4096]{2,1,0:T(8,128)(2,1)}, bf16[3,128,4096]{2,1,0:T(8,128)(2,1)S(1)}, u32[]{:S(2)}) copy-start(bf16[3,128,4096]{2,1,0:T(8,128)(2,1)S(1)} %get-tuple-element.241) | copy-start | bytes 9437188
  814.8 76.4 %all-to-all-start.6 = ((bf16[3,128,32,128]{3,1,0,2:T(8,128)(2,1)}), bf16[3,128,32,128]{3,1,0,2:T(8,128)(2,1)S(1)}, u32[]{:S(2)}, u32[]{:S(2)}) async-start(bf16[3,128,32,128]{3,1,0,2:T(8,128)(2,1)} %copy.73), calls=%async_computation.6 | async-start | bytes 6291456 | tf_op jit(solution)/shard_map/all_to_all | solution.py:61
  819.9 22.9 %copy-start.22 = (bf16[3,128,4096]{2,1,0:T(8,128)(2,1)S(1)}, bf16[3,128,4096]{2,1,0:T(8,128)(2,1)}, u32[]{:S(2)}) copy-start(bf16[3,128,4096]{2,1,0:T(8,128)(2,1)} %copy-done.21) | copy-start | bytes 9437188
  842.8 21.8 %copy-start.8 = (f32[128,64]{0,1:T(8,128)S(1)}, f32[128,64]{0,1:T(8,128)}, u32[]{:S(2)}) copy-start(f32[128,64]{0,1:T(8,128)} %copy-done.7) | copy-start | bytes 98308
  842.8 21.8 %copy-start.11 = (f32[128,64]{0,1:T(8,128)S(1)}, f32[128,64]{0,1:T(8,128)}, u32[]{:S(2)}) copy-start(f32[128,64]{0,1:T(8,128)} %copy-done.10) | copy-start | bytes 98308
  891.2 75.7 %all-to-all-start.5 = ((bf16[3,128,32,128]{1,3,0,2:T(8,128)(2,1)}), bf16[3,128,32,128]{1,3,0,2:T(8,128)(2,1)}, u32[]{:S(2)}, u32[]{:S(2)}) async-start(bf16[3,128,32,128]{1,3,0,2:T(8,128)(2,1)} %copy.70), calls=%async_computation.5 | async-start | bytes 6291456 | tf_op jit(solution)/shard_map/all_to_all | solution.py:60
  966.9 75.9 %all-to-all-start.4 = ((bf16[3,128,32,128]{1,3,0,2:T(8,128)(2,1)}), bf16[3,128,32,128]{1,3,0,2:T(8,128)(2,1)}, u32[]{:S(2)}, u32[]{:S(2)}) async-start(bf16[3,128,32,128]{1,3,0,2:T(8,128)(2,1)} %copy.67), calls=%async_computation.4 | async-start | bytes 6291456 | tf_op jit(solution)/shard_map/all_to_all | solution.py:59
  1054.8 3.7 copy-start.2
  1068.8 3.7 copy-start.2
  1082.8 3.7 copy-start.2
  1096.8 3.7 copy-start.2
  1111.8 89.5 %all-to-all-start.7 = ((bf16[3,1024,4,128]{3,2,0,1:T(4,128)(2,1)}), bf16[3,1024,4,128]{3,2,0,1:T(4,128)(2,1)S(1)}, u32[]{:S(2)}, u32[]{:S(2)}) async-start(bf16[3,1024,4,128]{3,2,0,1:T(4,128)(2,1)} %copy.76), calls=%async_computation.7 | async-start | bytes 6291456 | tf_op jit(solution)/shard_map/all_to_all | solution.py:66
  1201.3 1.9 copy-start.23
  1203.2 19.7 %copy-start.17 = (f32[1,4096]{1,0:T(1,128)S(1)}, f32[1,4096]{1,0:T(1,128)}, u32[]{:S(2)}) copy-start(f32[1,4096]{1,0:T(1,128)} %get-tuple-element.226) | copy-start | bytes 49156
  1271.9 43.7 %copy-start.14 = (f32[1,4096]{1,0:T(1,128)S(1)}, f32[1,4096]{1,0:T(1,128)}, u32[]{:S(2)}) copy-start(f32[1,4096]{1,0:T(1,128)} %get-tuple-element.229) | copy-start | bytes 49156
  1315.6 19.2 %copy-start.24 = (bf16[3,128,4096]{2,1,0:T(8,128)(2,1)}, bf16[3,128,4096]{2,1,0:T(8,128)(2,1)S(1)}, u32[]{:S(2)}) copy-start(bf16[3,128,4096]{2,1,0:T(8,128)(2,1)S(1)} %get-tuple-element.245) | copy-start | bytes 9437188
  1336.7 76.4 %all-to-all-start.10 = ((bf16[3,128,32,128]{3,1,0,2:T(8,128)(2,1)}), bf16[3,128,32,128]{3,1,0,2:T(8,128)(2,1)S(1)}, u32[]{:S(2)}, u32[]{:S(2)}) async-start(bf16[3,128,32,128]{3,1,0,2:T(8,128)(2,1)} %copy.86), calls=%async_computation.10 | async-start | bytes 6291456 | tf_op jit(solution)/shard_map/all_to_all | solution.py:61
  1341.7 22.9 %copy-start.25 = (bf16[3,128,4096]{2,1,0:T(8,128)(2,1)S(1)}, bf16[3,128,4096]{2,1,0:T(8,128)(2,1)}, u32[]{:S(2)}) copy-start(bf16[3,128,4096]{2,1,0:T(8,128)(2,1)} %copy-done.24) | copy-start | bytes 9437188
  1364.6 21.8 %copy-start.9 = (f32[128,64]{0,1:T(8,128)S(1)}, f32[128,64]{0,1:T(8,128)}, u32[]{:S(2)}) copy-start(f32[128,64]{0,1:T(8,128)} %copy-done.7) | copy-start | bytes 98308
  1364.6 21.8 %copy-start.12 = (f32[128,64]{0,1:T(8,128)S(1)}, f32[128,64]{0,1:T(8,128)}, u32[]{:S(2)}) copy-start(f32[128,64]{0,1:T(8,128)} %copy-done.10) | copy-start | bytes 98308
  1413.1 75.7 %all-to-all-start.9 = ((bf16[3,128,32,128]{1,3,0,2:T(8,128)(2,1)}), bf16[3,128,32,128]{1,3,0,2:T(8,128)(2,1)}, u32[]{:S(2)}, u32[]{:S(2)}) async-start(bf16[3,128,32,128]{1,3,0,2:T(8,128)(2,1)} %copy.83), calls=%async_computation.9 | async-start | bytes 6291456 | tf_op jit(solution)/shard_map/all_to_all | solution.py:60
  1488.7 75.9 %all-to-all-start.8 = ((bf16[3,128,32,128]{1,3,0,2:T(8,128)(2,1)}), bf16[3,128,32,128]{1,3,0,2:T(8,128)(2,1)}, u32[]{:S(2)}, u32[]{:S(2)}) async-start(bf16[3,128,32,128]{1,3,0,2:T(8,128)(2,1)} %copy.80), calls=%async_computation.8 | async-start | bytes 6291456 | tf_op jit(solution)/shard_map/all_to_all | solution.py:59
  1576.8 3.7 copy-start.1
  1590.8 3.7 copy-start.1
  1604.9 3.7 copy-start.1
  1619.0 3.7 copy-start.1
  1708.0 1.9 copy-start.26
  1709.8 18.0 copy-start.15
  (1 other events, 1.7 us)
where the time goes:
time: 1830 us; the launch traced here: 1820 us
  matrix products  627 us (34%)
  local copies, waits for them, and re-layouts  543 us (30%)
  waiting for transfers between devices  438 us (24%)
  blocking collectives  75.7 us (4%)
  other arithmetic  65.1 us (4%)
  starting transfers between devices  62.6 us (3%)
    unnamed x58, local copies, waits for them, and re-layouts  263 us
    all_to_all x3, waiting for transfers between devices, layer_step(): k_all = lax.all_to_all(k_loc, 'seq', 2, 1, tiled=True)  201 us
    dot_general x3, matrix products, layer_step(): jnp.einsum('bsd,df->bsf', normed_mlp, w_up, preferred_element_type=jnp.fl...  147 us
    all_to_all x3, waiting for transfers between devices, layer_step(): q_all = lax.all_to_all(q_loc, 'seq', 2, 1, tiled=True)  132 us
    dot_general x3, matrix products, layer_step(): jnp.einsum('bsf,fd->bsd', gelu_act, w_down, preferred_element_type=jnp.fl...  131 us
    all_to_all x3, waiting for transfers between devices, layer_step(): v_all = lax.all_to_all(v_loc, 'seq', 2, 1, tiled=True)  105 us
    all_to_all x1, blocking collectives, layer_step(): attn_loc = lax.all_to_all(attn_heads, 'seq', 1, 2, tiled=True)  75.7 us
    dot_general x3, matrix products, layer_step(): jnp.einsum('bsd,dhe->bshe', normed, w_query, preferred_element_type=jnp.f...  67.5 us
  transfers between devices with their start and end apart: 11, of which 8 were waited for; matrix products, arithmetic and copies ran while one was open for 21% of the time, Pallas kernels for 0%

commit v1 on v0

v1 whole, which is shorter than its diff:
```python
import functools

import jax
import jax.numpy as jnp
from jax import lax
from jax.experimental import pallas as pl
from jax.experimental.pallas import tpu as pltpu
from jax.sharding import PartitionSpec as P

ROPE_BASE = 10000.0
NORM_EPS = 1e-6
NEG = -1e30
LOG2E = 1.4426950408889634
F32 = jnp.float32
BF16 = jnp.bfloat16
MESH = pl.DeviceIdType.MESH

ROUTE = (
    ((0, 0), (1, 1), (2, 0)),
    ((1, 0), (1, 2), (3, 0)),
    ((0, 1), (2, 1), (3, 1)),
    ((0, 2), (2, 2), (3, 2)),
)
SEND_ORDER = ((1, 2), (2,), (0, 2), (1, 0))
HOME = tuple(
    tuple(next((i, q) for i in range(4) for q in range(3) if ROUTE[i][q] == (c, s)) for s in range(3))
    for c in range(4)
)
KV_SENDS = (((0, 1, 0),), ((1, 2, 0), (2, 2, 1), (0, 0, 0)), ((0, 3, 0),), ())

ROWS = 128
TOK = 3 * ROWS
TN = 1024
HG = 8


def dot(a, b):
    return jnp.dot(a, b, preferred_element_type=F32)


def gelu_tanh(x):
    c0 = 0.7978845608028654
    t = jnp.tanh(x * (c0 + (c0 * 0.044715) * (x * x)))
    h = 0.5 * x
    return h + h * t


def layers_kernel(
    n_layers, d_model, ff,
    x_ref, tab_ref, ga_ref, gm_ref, wq_ref, wk_ref, wv_ref, wo_ref, wu_ref, wd_ref,
    y_ref,
    hbuf, nbuf, pbuf, rbuf, obuf, acc, mask, ring, qring,
    wsem, qsem, xs_sem, xr_sem, ns_sem, nr_sem, ks_sem, kr_sem, os_sem, or_sem, ys_sem, yr_sem, cred,
):
    me = lax.axis_index("seq")
    core = lax.rem(me, 2)
    chip = me // 2
    partner = {"seq": me + 1 - 2 * core}

    n_out = d_model // TN
    n_up = -(-ff // TN)
    tail = ff - (n_up - 1) * TN
    k_units = ff // 256
    cuts = [0, (k_units // 3) * 256, 2 * (k_units // 3) * 256, ff]
    tiles = n_out + n_up + 3 * n_out
    o_rows = 4 * TN

    def on_chip(c):
        return {"seq": 2 * c + core}

    def cols(i):
        return pl.ds(pl.multiple_of(i * TN, TN), TN)

    def q_copy(l, i):
        w = (wk_ref, wv_ref)
        return w, l, i

    def q_start(l, i):
        for kind, ref in enumerate((wk_ref, wv_ref, wq_ref)):
            for g in range(2):
                idx = 2 * g + kind if kind < 2 else 4 + g

                @pl.when(i == idx)
                def _(ref=ref, g=g, idx=idx):
                    heads = pl.ds(pl.multiple_of(core * 2 * HG + g * HG, HG), HG)
                    pltpu.make_async_copy(ref.at[l, :, heads, :], qring.at[idx % 2], qsem.at[idx % 2]).start()

    def q_wait(slot):
        pltpu.make_async_copy(wq_ref.at[0, :, pl.ds(0, HG), :], qring.at[slot], qsem.at[slot]).wait()

    def t_slot(l, t):
        return lax.rem(l * tiles + t, 2)

    def out_copy(l, i):
        s = t_slot(l, i)
        return pltpu.make_async_copy(wo_ref.at[l, :, cols(i)], ring.at[s, pl.ds(0, o_rows)], wsem.at[s])

    def up_copy(l, i):
        s = t_slot(l, n_out + i)
        return pltpu.make_async_copy(wu_ref.at[l, :, cols(i)], ring.at[s, pl.ds(0, d_model)], wsem.at[s])

    def up_tail_copy(l):
        s = t_slot(l, n_out + n_up - 1)
        src = wu_ref.at[l, :, pl.ds((n_up - 1) * TN, tail)]
        return pltpu.make_async_copy(src, ring.at[s, pl.ds(0, d_model), pl.ds(0, tail)], wsem.at[s])

    def down_copy(l, n, kk):
        s = t_slot(l, n_out + n_up + 3 * n + kk)
        size = cuts[kk + 1] - cuts[kk]
        return pltpu.make_async_copy(
            wd_ref.at[l, pl.ds(cuts[kk], size), cols(n)], ring.at[s, pl.ds(0, size)], wsem.at[s])

    q_start(0, 0)
    out_copy(0, 0).start()

    barrier = pltpu.get_barrier_semaphore()
    for k in range(1, 8):
        pl.semaphore_signal(barrier, inc=1, device_id={"seq": lax.rem(me + k, 8)}, device_id_type=MESH)
    pl.semaphore_wait(barrier, 7)

    def rows(t):
        return pl.ds(t * ROWS, ROWS)

    for c in range(4):
        @pl.when(chip == c)
        def _(c=c):
            for k, q in enumerate(SEND_ORDER[c]):
                dst, slot = ROUTE[c][q]
                pltpu.make_async_remote_copy(
                    src_ref=x_ref.at[q], dst_ref=hbuf.at[rows(slot)], send_sem=xs_sem.at[k],
                    recv_sem=xr_sem.at[slot], device_id=on_chip(dst), device_id_type=MESH).start()
            for q in range(3):
                dst, slot = ROUTE[c][q]
                if dst == c:
                    pltpu.make_async_copy(x_ref.at[q], hbuf.at[rows(slot)], xr_sem.at[slot]).start()

    ri = lax.broadcasted_iota(jnp.int32, (2 * ROWS, 2 * ROWS), 0)
    ci = lax.broadcasted_iota(jnp.int32, (2 * ROWS, 2 * ROWS), 1)
    flip = core * ROWS
    rp = jnp.where(ri < ROWS, ri + flip, ri - flip)
    cp = jnp.where(ci < ROWS, ci + flip, ci - flip)
    mask[...] = jnp.where(cp <= rp, 0.0, NEG)

    def norm_rows(gain, t):
        def step(i, _):
            r = pl.ds(pl.multiple_of(t * ROWS + i * 16, 16), 16)
            v = hbuf[r, :].astype(F32)
            scale = lax.rsqrt(jnp.mean(v * v, axis=1, keepdims=True) + NORM_EPS)
            nbuf[0, r, :] = (v * scale * gain).astype(BF16)
            return 0

        lax.fori_loop(0, ROWS // 16, step, 0)

    def n_send(t):
        return pltpu.make_async_remote_copy(
            src_ref=nbuf.at[0, rows(t)], dst_ref=nbuf.at[1, rows(t)], send_sem=ns_sem.at[t],
            recv_sem=nr_sem.at[t], device_id=partner, device_id_type=MESH)

    def kv_send(i, s, k, slot, dst, rslot):
        base = 4 + 4 * (i % 2) + 2 * (i // 2) if isinstance(i, int) else 4 + 4 * lax.rem(i, 2) + 2 * (i // 2)
        return pltpu.make_async_remote_copy(
            src_ref=pbuf.at[base + s, rows(slot)], dst_ref=rbuf.at[i, rslot, s], send_sem=ks_sem.at[i, s, k],
            recv_sem=kr_sem.at[i, rslot, s], device_id=on_chip(dst), device_id_type=MESH)

    def kv_wait(i, s, rslot):
        pltpu.make_async_remote_copy(
            src_ref=pbuf.at[0, rows(0)], dst_ref=rbuf.at[i, rslot, s], send_sem=ks_sem.at[i, s, 0],
            recv_sem=kr_sem.at[i, rslot, s], device_id=partner, device_id_type=MESH).wait_recv()

    def o_send(g):
        piece = core * 2 + g
        return pltpu.make_async_remote_copy(
            src_ref=pbuf.at[2 * g + 1], dst_ref=obuf.at[piece], send_sem=os_sem.at[g],
            recv_sem=or_sem.at[g], device_id=partner, device_id_type=MESH)

    def layer(l, _):
        gain = ga_ref[l]
        for t in range(3):
            @pl.when(l == 0)
            def _(t=t):
                pltpu.make_async_copy(x_ref.at[0], hbuf.at[rows(t)], xr_sem.at[t]).wait()

            norm_rows(gain, t)
            if t > 0:
                n_send(t - 1).start()

        def qkv_tile(i, _):
            slot = lax.rem(i, 2)
            q_wait(slot)

            @pl.when(i < 5)
            def _():
                q_start(l, i + 1)

            @pl.when(jnp.logical_and(i == 5, l < n_layers - 1))
            def _():
                q_start(l + 1, 0)

            def side(s, _):
                b = 2 * i + s

                @pl.when(b == 0)
                def _():
                    n_send(2).start()

                @pl.when(b == 1)
                def _():
                    for t in range(3):
                        n_send(t).wait_recv()

                    @pl.when(l > 0)
                    def _():
                        for c in range(4):
                            @pl.when(chip == c)
                            def _(c=c):
                                for k in sorted({1 if dst == 2 else 0 for _, dst, _ in KV_SENDS[c]}):
                                    pl.semaphore_wait(cred.at[k], 1)

                @pl.when(jnp.logical_and(b >= 1, b <= 8))
                def _():
                    pi = (b - 1) // 2
                    ps = lax.rem(b - 1, 2)
                    for c in range(4):
                        @pl.when(chip == c)
                        def _(c=c):
                            for k, (sl, dst, rs) in enumerate(KV_SENDS[c]):
                                kv_send(pi, ps, k, sl, dst, rs).start()

                kq = d_model // 8
                u = functools.reduce(jnp.add, [
                    dot(nbuf[s, :, j * kq:(j + 1) * kq], qring[slot, j * kq:(j + 1) * kq].reshape(kq, TN))
                    for j in range(8)])
                piece = jnp.where(i < 4, 4 + 4 * lax.rem(i, 2) + 2 * (i // 2), 2 * (i - 4)) + s
                plain = jnp.logical_and(lax.rem(i, 2) == 1, i < 4)
                cos = jnp.where(plain, 1.0, tab_ref[0, s])
                sin = jnp.where(plain, 0.0, tab_ref[1, s])
                for h in range(HG):
                    uh = u[:, h * 128:(h + 1) * 128]
                    pbuf[piece, :, h * 128:(h + 1) * 128] = (
                        uh * cos + pltpu.roll(uh, 64, axis=1) * sin).astype(BF16)

                @pl.when(jnp.logical_and(i < 4, chip != 2))
                def _():
                    rbuf[jnp.minimum(i, 3), 1, s] = pbuf[piece, 0:ROWS, :]

                return 0

            lax.fori_loop(0, 2, side, 0)
            return 0

        lax.fori_loop(0, 6, qkv_tile, 0)
        for t in range(3):
            n_send(t).wait_send()

        bias0 = jnp.where(lax.rem(chip, 2) == 1, 0.0, NEG)
        bias1 = jnp.where(chip == 1, NEG, 0.0)
        c2 = 128 ** -0.5 * LOG2E

        def group(g, _):
            for j in range(2):
                for s in range(2):
                    kv_wait(2 * g + j, s, 0)

            @pl.when(chip == 2)
            def _():
                for j in range(2):
                    for s in range(2):
                        kv_wait(2 * g + j, s, 1)

            @pl.when(g == 1)
            def _():
                o_send(0).start()

            def head(h, _):
                lanes = pl.ds(pl.multiple_of(h * 128, 128), 128)

                def local(base, t):
                    r = rows(t)
                    return jnp.concatenate([pbuf[base + 2 * g, r, lanes], pbuf[base + 2 * g + 1, r, lanes]], axis=0)

                def remote(j, rs):
                    return jnp.concatenate([rbuf[2 * g + j, rs, 0, :, lanes], rbuf[2 * g + j, rs, 1, :, lanes]], axis=0)

                for t in range(3):
                    q = local(0, t)
                    blocks = [(remote(0, 0), remote(1, 0), bias0 if t == 0 else bias1)]
                    if t > 0:
                        blocks.append((remote(0, 1), remote(1, 1), bias1))
                    if t == 2:
                        blocks.append((local(4, 1), local(8, 1), None))
                    blocks.append((local(4, t), local(8, t), mask[...]))
                    xs = []
                    for k, _, b in blocks:
                        sc = lax.dot_general(q, k, (((1,), (1,)), ((), ())), preferred_element_type=F32) * c2
                        xs.append(sc if b is None else sc + b)
                    top = functools.reduce(jnp.maximum, xs)
                    top = jnp.max(top, axis=1, keepdims=True)
                    es = [jnp.exp2(v - top) for v in xs]
                    total = jnp.sum(functools.reduce(jnp.add, es), axis=1, keepdims=True)
                    o = functools.reduce(jnp.add, [dot(e.astype(BF16), v) for e, (_, v, _) in zip(es, blocks)])
                    o = (o * (1.0 / total)).astype(BF16)
                    obuf[core * 2 + g, rows(t), lanes] = o[:ROWS]
                    pbuf[2 * g + 1, rows(t), lanes] = o[ROWS:]
                return 0

            lax.fori_loop(0, HG, head, 0)
            return 0

        lax.fori_loop(0, 2, group, 0)

        for c in range(4):
            @pl.when(chip == c)
            def _(c=c):
                for i in range(4):
                    for s in range(2):
                        for k, (sl, dst, rs) in enumerate(KV_SENDS[c]):
                            kv_send(i, s, k, sl, dst, rs).wait_send()

                @pl.when(l < n_layers - 1)
                def _():
                    src, k = ((1, 0), (0, 0), (1, 1), (2, 0))[c]
                    pl.semaphore_signal(cred.at[k], inc=1, device_id=on_chip(src), device_id_type=MESH)

        o_send(1).start()
        for g in range(2):
            o_send(g).wait_recv()

        def out_tile(i, _):
            out_copy(l, i).wait()

            @pl.when(i < n_out - 1)
            def _():
                out_copy(l, i + 1).start()

            @pl.when(i == n_out - 1)
            def _():
                up_copy(l, 0).start()

            slot = t_slot(l, i)
            u = functools.reduce(
                jnp.add, [dot(obuf[j], ring[slot, j * TN:(j + 1) * TN, :]) for j in range(4)])
            hbuf[:, cols(i)] = (hbuf[:, cols(i)].astype(F32) + u).astype(BF16)
            return 0

        lax.fori_loop(0, n_out, out_tile, 0)
        for g in range(2):
            o_send(g).wait_send()

        gain_m = gm_ref[l]
        for t in range(3):
            norm_rows(gain_m, t)

        def up_tile(i, _):
            @pl.when(i < n_up - 1)
            def _():
                up_copy(l, i).wait()

            @pl.when(i == n_up - 1)
            def _():
                up_tail_copy(l).wait()

            @pl.when(i < n_up - 2)
            def _():
                up_copy(l, i + 1).start()

            @pl.when(i == n_up - 2)
            def _():
                up_tail_copy(l).start()

            @pl.when(i == n_up - 1)
            def _():
                down_copy(l, 0, 0).start()

            slot = t_slot(l, n_out + i)
            pbuf[i] = gelu_tanh(dot(nbuf[0], ring[slot, 0:d_model, :])).astype(BF16)
            return 0

        lax.fori_loop(0, n_up, up_tile, 0)

        def y_send(c, t, n):
            dst, q = HOME[c][t]
            if dst == c:
                return pltpu.make_async_copy(hbuf.at[rows(t), cols(n)], y_ref.at[q, :, cols(n)], yr_sem.at[q, n])
            return pltpu.make_async_remote_copy(
                src_ref=hbuf.at[rows(t), cols(n)], dst_ref=y_ref.at[q, :, cols(n)], send_sem=ys_sem.at[t, n],
                recv_sem=yr_sem.at[q, n], device_id=on_chip(dst), device_id_type=MESH)

        def y_start(n):
            for c in range(4):
                @pl.when(chip == c)
                def _(c=c):
                    for t in range(3):
                        y_send(c, t, n).start()

        def down_tile(n, _):
            for kk in range(3):
                down_copy(l, n, kk).wait()
                if kk < 2:
                    down_copy(l, n, kk + 1).start()
                else:
                    @pl.when(n < n_out - 1)
                    def _():
                        down_copy(l, n + 1, 0).start()

                    @pl.when(jnp.logical_and(n == n_out - 1, l < n_layers - 1))
                    def _():
                        out_copy(l + 1, 0).start()

                if kk == 0:
                    @pl.when(jnp.logical_and(n > 0, l == n_layers - 1))
                    def _():
                        y_start(n - 1)

                slot = t_slot(l, n_out + n_up + 3 * n + kk)
                parts = []
                lo = cuts[kk]
                while lo < cuts[kk + 1]:
                    hi = min((lo // TN + 1) * TN, cuts[kk + 1])
                    parts.append(dot(pbuf[lo // TN, :, lo % TN:lo % TN + hi - lo],
                                     ring[slot, lo - cuts[kk]:hi - cuts[kk], :]))
                    lo = hi
                u = functools.reduce(jnp.add, parts)
                if kk == 0:
                    acc[...] = u
                elif kk == 1:
                    acc[...] += u
                else:
                    hbuf[:, cols(n)] = (hbuf[:, cols(n)].astype(F32) + (acc[...] + u)).astype(BF16)
            return 0

        lax.fori_loop(0, n_out, down_tile, 0)

        @pl.when(l == n_layers - 1)
        def _():
            for c in range(4):
                @pl.when(chip == c)
                def _(c=c):
                    for k, q in enumerate(SEND_ORDER[c]):
                        dst, slot = ROUTE[c][q]
                        pltpu.make_async_remote_copy(
                            src_ref=x_ref.at[q], dst_ref=hbuf.at[rows(slot)], send_sem=xs_sem.at[k],
                            recv_sem=xr_sem.at[slot], device_id=on_chip(dst), device_id_type=MESH).wait_send()
            y_start(n_out - 1)
            for c in range(4):
                @pl.when(chip == c)
                def _(c=c):
                    for n in range(n_out):
                        for t in range(3):
                            if HOME[c][t][0] != c:
                                y_send(c, t, n).wait_send()
            for n in range(n_out):
                for q in range(3):
                    pltpu.make_async_copy(hbuf.at[rows(0), cols(n)], y_ref.at[q, :, cols(n)], yr_sem.at[q, n]).wait()

        return 0

    lax.fori_loop(0, n_layers, layer, 0)


def run_layers(x_loc, tab, g_attn, g_mlp, w_query, w_key, w_value, w_out, w_up, w_down):
    n_layers, d_model = g_attn.shape
    ff = w_up.shape[-1]
    n_out = d_model // TN
    k_units = ff // 256
    ring_rows = max(4 * TN, d_model, (k_units - 2 * (k_units // 3)) * 256)
    vmem = pl.BlockSpec(memory_space=pltpu.VMEM)
    hbm = pl.BlockSpec(memory_space=pl.ANY)
    dma = pltpu.SemaphoreType.DMA
    n_pieces = max(12, -(-ff // TN))
    return pl.pallas_call(
        functools.partial(layers_kernel, n_layers, d_model, ff),
        out_shape=jax.ShapeDtypeStruct(x_loc.shape, BF16),
        in_specs=[hbm, vmem, vmem, vmem] + [hbm] * 6,
        out_specs=hbm,
        scratch_shapes=[
            pltpu.VMEM((TOK, d_model), BF16),
            pltpu.VMEM((2, TOK, d_model), BF16),
            pltpu.VMEM((n_pieces, TOK, TN), BF16),
            pltpu.VMEM((4, 2, 2, ROWS, TN), BF16),
            pltpu.VMEM((4, TOK, TN), BF16),
            pltpu.VMEM((TOK, TN), F32),
            pltpu.VMEM((2 * ROWS, 2 * ROWS), F32),
            pltpu.VMEM((2, ring_rows, TN), BF16),
            pltpu.VMEM((2, d_model, HG, 128), BF16),
            dma((2,)), dma((2,)), dma((2,)), dma((3,)), dma((3,)), dma((3,)),
            dma((4, 2, 3)), dma((4, 2, 2)), dma((2,)), dma((2,)), dma((3, n_out)), dma((3, n_out)),
            pltpu.SemaphoreType.REGULAR((2,)),
        ],
        compiler_params=pltpu.CompilerParams(
            collective_id=0, has_side_effects=True, vmem_limit_bytes=67043328),
        name="layers",
    )(x_loc, tab, g_attn.reshape(n_layers, 1, d_model), g_mlp.reshape(n_layers, 1, d_model),
      w_query, w_key, w_value, w_out.reshape(n_layers, -1, d_model), w_up, w_down)


def rope_tables(pos_loc):
    me = lax.axis_index("seq")
    core, chip = me % 2, me // 2
    pos_all = lax.all_gather(pos_loc, "seq")
    home = jnp.array([[HOME[c][s][0] for s in range(3)] for c in range(4)], jnp.int32)
    chunk = lax.dynamic_index_in_dim(home, chip, 0, keepdims=False)
    side = jnp.stack([core, 1 - core])
    pos = pos_all[(2 * chunk[None, :] + side[:, None])].reshape(2, TOK)
    inv_freq = ROPE_BASE ** (-jnp.arange(64, dtype=F32) * (2.0 / 128))
    angles = pos.astype(F32)[..., None] * inv_freq
    cos, sin = jnp.cos(angles), jnp.sin(angles)
    return jnp.stack([jnp.concatenate([cos, cos], -1), jnp.concatenate([-sin, sin], -1)])


def solution(mesh):
    tok_spec = P(None, ("data", "seq"), None)
    in_specs = (tok_spec, P(("data", "seq"))) + (P(),) * 8

    def device_fn(x_loc, pos_loc, w_query, w_key, w_value, w_out, w_up, w_down, g_attn, g_mlp):
        tab = rope_tables(pos_loc)
        return run_layers(x_loc, tab, g_attn, g_mlp, w_query, w_key, w_value, w_out, w_up, w_down)

    return jax.shard_map(device_fn, mesh=mesh, in_specs=in_specs, out_specs=tok_spec, check_vma=False)
```

time: 1830 us -> 677 us (0.37)
  Pallas kernels: 0 us -> 651 us
  matrix products: 627 us -> 0 us
  local copies, waits for them, and re-layouts: 543 us -> 7.54 us
  waiting for transfers between devices: 438 us -> 0 us
  starting transfers between devices: 62.6 us -> 0 us
  blocking collectives: 75.7 us -> 13.5 us
  other arithmetic: 65.1 us -> 3.5 us
    pallas_call x0 -> x1, Pallas kernels: none -> 651 us  [run_layers(): pl.pallas_call(functools.partial(layers_kernel, n_layers, d_model, ff), o...]
    dot_general x42 -> x0, matrix products: 627 us -> none  [the longest x3 147 us: layer_step(): jnp.einsum('bsd,df->bsf', normed_mlp, w_up, preferred_element_type=jnp.fl...]
    all_to_all x11 -> x0, waiting for transfers between devices: 438 us -> none  [the longest x3 201 us: layer_step(): k_all = lax.all_to_all(k_loc, 'seq', 2, 1, tiled=True)]
    unnamed x58 -> x1, local copies, waits for them, and re-layouts: 263 us -> 3.91 us
    slice x5 -> x0, local copies, waits for them, and re-layouts: 197 us -> none  [the longest x1 64.9 us: device_fn(): w_key[layer_idx]]
    all_to_all x1 -> x0, blocking collectives: 75.7 us -> none  [layer_step(): attn_loc = lax.all_to_all(attn_heads, 'seq', 1, 2, tiled=True)]
    all_to_all x11 -> x0, starting transfers between devices: 62.6 us -> none  [the longest x3 25.5 us: layer_step(): k_all = lax.all_to_all(k_loc, 'seq', 2, 1, tiled=True)]
    reduce_sum x13 -> x0, other arithmetic: 44.8 us -> none  [the longest x12 44.2 us: one_block(): row_sum = jnp.sum(exp_f32, axis=-1)]
  transfers between devices with their start and end apart: 11 -> 0, of which waited for: 8 -> 0; matrix products, arithmetic and copies ran while one was open for 21% -> 0% of each run, Pallas kernels for 0% -> 0%
where the time goes in v1:
time: 677 us; the launch traced here: 676 us
  Pallas kernels  651 us (96%)
  blocking collectives  13.5 us (2%)
  local copies, waits for them, and re-layouts  7.54 us (1%)
    pallas_call x1, Pallas kernels, run_layers(): pl.pallas_call(functools.partial(layers_kernel, n_layers, d_model, ff), o...  651 us

profile of v1, /device:TPU:0, one launch (start us, length us, event | category | flops | bytes accessed | tf_op | source)
XLA Modules:
  0.0 675.5 jit_solution(2698419858076674861)
XLA Ops:
  0.0 0.1 pad_add_fusion
  0.1 0.7 multiply_bitcast_fusion
  0.8 0.1 compare_select_fusion
  0.8 0.1 reshape.89
  0.9 13.5 %all-gather.1 = s32[8,1,128]{2,1,0:T(1,128)S(1)} all-gather(s32[1,1,128]{2,1,0:T(1,128)} %bitcast.14), channel_id=2, replica_groups=mesh['data'=4,'seq'=8] {'seq'}, dimensions={0}, use_global_device_ids=true | all-gather | bytes 4608 | tf_op jit(solution)/shard_map/all_gather | solution.py:499
  14.5 0.6 gather_fusion
  15.0 1.5 reshape.84.ga_ref
  16.5 1.5 reshape.85.gm_ref
  18.0 1.4 multiply_cosine_fusion
  19.5 0.3 maximum_bitcast_fusion
  19.8 0.9 pad_maximum_fusion.tab_ref
  20.7 650.9 %layers.1 = bf16[3,128,4096]{2,1,0:T(8,128)(2,1)} custom-call(bf16[3,128,4096]{2,1,0:T(8,128)(2,1)} %x_ref.1, f32[2,2,384,128]{3,2,1,0:T(8,128)} %pad_maximum_fusion.tab_ref, f32[3,1,4096]{2,1,0:T(1,128)} %reshape.84.ga_ref, f32[3,1,4096]{2,1,0:T(1,128)} %reshape.85.gm_ref, bf16[3,4096,32,128]{3,2,1,0:T(8,128)(2,1)} %wq_ref.1, ...), custom_call_target="tpu_custom_call" | custom-call | tf_op jit(solution)/shard_map/layers/pallas_call | solution.py:470
  671.6 3.9 copy.14
  (4 shorter events, 0.0 us)

commit v2 on v1

--- a/solution.py
+++ b/solution.py
@@ -31,6 +31,8 @@
 ROWS = 128
 TOK = 3 * ROWS
 TN = 1024
+TH = 512
+SLOTS = 5
 HG = 8
 
 
@@ -47,10 +49,11 @@
 
 def layers_kernel(
     n_layers, d_model, ff,
-    x_ref, tab_ref, ga_ref, gm_ref, wq_ref, wk_ref, wv_ref, wo_ref, wu_ref, wd_ref,
+    x_ref, cs_ref, ga_ref, gm_ref, wq_ref, wk_ref, wv_ref, wo_ref, wu_ref, wd_ref,
     y_ref,
-    hbuf, nbuf, pbuf, rbuf, obuf, acc, mask, ring, qring,
-    wsem, qsem, xs_sem, xr_sem, ns_sem, nr_sem, ks_sem, kr_sem, os_sem, or_sem, ys_sem, yr_sem, cred,
+    hbuf, nbuf, pbuf, rbuf, obuf, tab, mask, ring, qring,
+    wsem, qsem, xs_sem, xr_sem, ts_sem, tr_sem, ps_sem, pr_sem, ns_sem, nr_sem, ks_sem, kr_sem, os_sem, or_sem,
+    ys_sem, yr_sem, cred,
 ):
     me = lax.axis_index("seq")
     core = lax.rem(me, 2)
@@ -59,10 +62,12 @@
 
     n_out = d_model // TN
     n_up = -(-ff // TN)
-    tail = ff - (n_up - 1) * TN
+    n_col = d_model // TH
+    up_tiles = 2 * n_up
+    tail = ff - (n_up * TN - TH)
     k_units = ff // 256
     cuts = [0, (k_units // 3) * 256, 2 * (k_units // 3) * 256, ff]
-    tiles = n_out + n_up + 3 * n_out
+    tiles = 2 * n_out + up_tiles + 6 * n_out
     o_rows = 4 * TN
 
     def on_chip(c):
@@ -71,9 +76,8 @@
     def cols(i):
         return pl.ds(pl.multiple_of(i * TN, TN), TN)
 
-    def q_copy(l, i):
-        w = (wk_ref, wv_ref)
-        return w, l, i
+    def half(i):
+        return pl.ds(pl.multiple_of(i * TH, TH), TH)
 
     def q_start(l, i):
         for kind, ref in enumerate((wk_ref, wv_ref, wq_ref)):
@@ -89,29 +93,44 @@
         pltpu.make_async_copy(wq_ref.at[0, :, pl.ds(0, HG), :], qring.at[slot], qsem.at[slot]).wait()
 
     def t_slot(l, t):
-        return lax.rem(l * tiles + t, 2)
+        return lax.rem(l * tiles + t, SLOTS)
 
     def out_copy(l, i):
         s = t_slot(l, i)
-        return pltpu.make_async_copy(wo_ref.at[l, :, cols(i)], ring.at[s, pl.ds(0, o_rows)], wsem.at[s])
+        return pltpu.make_async_copy(wo_ref.at[l, :, half(i)], ring.at[s, pl.ds(0, o_rows)], wsem.at[s])
 
     def up_copy(l, i):
-        s = t_slot(l, n_out + i)
-        return pltpu.make_async_copy(wu_ref.at[l, :, cols(i)], ring.at[s, pl.ds(0, d_model)], wsem.at[s])
+        s = t_slot(l, 2 * n_out + i)
+        return pltpu.make_async_copy(wu_ref.at[l, :, half(i)], ring.at[s, pl.ds(0, d_model)], wsem.at[s])
 
     def up_tail_copy(l):
-        s = t_slot(l, n_out + n_up - 1)
-        src = wu_ref.at[l, :, pl.ds((n_up - 1) * TN, tail)]
+        s = t_slot(l, 2 * n_out + up_tiles - 1)
+        src = wu_ref.at[l, :, pl.ds((up_tiles - 1) * TH, tail)]
         return pltpu.make_async_copy(src, ring.at[s, pl.ds(0, d_model), pl.ds(0, tail)], wsem.at[s])
 
-    def down_copy(l, n, kk):
-        s = t_slot(l, n_out + n_up + 3 * n + kk)
+    def down_copy(l, n, kk, j):
+        s = t_slot(l, 2 * n_out + up_tiles + 6 * n + 2 * kk + j)
         size = cuts[kk + 1] - cuts[kk]
         return pltpu.make_async_copy(
-            wd_ref.at[l, pl.ds(cuts[kk], size), cols(n)], ring.at[s, pl.ds(0, size)], wsem.at[s])
+            wd_ref.at[l, pl.ds(cuts[kk], size), half(2 * n + j)], ring.at[s, pl.ds(0, size)], wsem.at[s])
+
+    def up_start(l, i):
+        @pl.when(i < up_tiles - 1)
+        def _():
+            up_copy(l, i).start()
+
+        @pl.when(i == up_tiles - 1)
+        def _():
+            up_tail_copy(l).start()
+
+        for d in range(3):
+            @pl.when(i == up_tiles + d)
+            def _(d=d):
+                down_copy(l, 0, d // 2, d % 2).start()
 
     q_start(0, 0)
-    out_copy(0, 0).start()
+    for i in range(3):
+        out_copy(0, i).start()
 
     barrier = pltpu.get_barrier_semaphore()
     for k in range(1, 8):
@@ -119,7 +138,18 @@
     pl.semaphore_wait(barrier, 7)
 
     def rows(t):
-        return pl.ds(t * ROWS, ROWS)
+        return pl.ds(t * ROWS if isinstance(t, int) else pl.multiple_of(t * ROWS, ROWS), ROWS)
+
+    def tab_send(c, k, q):
+        dst, slot = ROUTE[c][q]
+        return pltpu.make_async_remote_copy(
+            src_ref=cs_ref, dst_ref=tab.at[0, rows(slot)], send_sem=ts_sem.at[k],
+            recv_sem=tr_sem.at[slot], device_id=on_chip(dst), device_id_type=MESH)
+
+    def tab_pair(t):
+        return pltpu.make_async_remote_copy(
+            src_ref=tab.at[0, rows(t)], dst_ref=tab.at[1, rows(t)], send_sem=ps_sem.at[t],
+            recv_sem=pr_sem.at[t], device_id=partner, device_id_type=MESH)
 
     for c in range(4):
         @pl.when(chip == c)
@@ -129,10 +159,12 @@
                 pltpu.make_async_remote_copy(
                     src_ref=x_ref.at[q], dst_ref=hbuf.at[rows(slot)], send_sem=xs_sem.at[k],
                     recv_sem=xr_sem.at[slot], device_id=on_chip(dst), device_id_type=MESH).start()
+                tab_send(c, k, q).start()
             for q in range(3):
                 dst, slot = ROUTE[c][q]
                 if dst == c:
                     pltpu.make_async_copy(x_ref.at[q], hbuf.at[rows(slot)], xr_sem.at[slot]).start()
+                    pltpu.make_async_copy(cs_ref, tab.at[0, rows(slot)], tr_sem.at[slot]).start()
 
     ri = lax.broadcasted_iota(jnp.int32, (2 * ROWS, 2 * ROWS), 0)
     ci = lax.broadcasted_iota(jnp.int32, (2 * ROWS, 2 * ROWS), 1)
@@ -142,14 +174,11 @@
     mask[...] = jnp.where(cp <= rp, 0.0, NEG)
 
     def norm_rows(gain, t):
-        def step(i, _):
+        for i in range(ROWS // 16):
             r = pl.ds(pl.multiple_of(t * ROWS + i * 16, 16), 16)
             v = hbuf[r, :].astype(F32)
             scale = lax.rsqrt(jnp.mean(v * v, axis=1, keepdims=True) + NORM_EPS)
             nbuf[0, r, :] = (v * scale * gain).astype(BF16)
-            return 0
-
-        lax.fori_loop(0, ROWS // 16, step, 0)
 
     def n_send(t):
         return pltpu.make_async_remote_copy(
@@ -168,21 +197,28 @@
             recv_sem=kr_sem.at[i, rslot, s], device_id=partner, device_id_type=MESH).wait_recv()
 
     def o_send(g):
-        piece = core * 2 + g
         return pltpu.make_async_remote_copy(
-            src_ref=pbuf.at[2 * g + 1], dst_ref=obuf.at[piece], send_sem=os_sem.at[g],
+            src_ref=pbuf.at[2 * g + 1], dst_ref=obuf.at[g], send_sem=os_sem.at[g],
             recv_sem=or_sem.at[g], device_id=partner, device_id_type=MESH)
 
     def layer(l, _):
-        gain = ga_ref[l]
-        for t in range(3):
+        gain = ga_ref[pl.ds(l, 1), :]
+
+        def norm_chunk(t, _):
             @pl.when(l == 0)
-            def _(t=t):
+            def _():
                 pltpu.make_async_copy(x_ref.at[0], hbuf.at[rows(t)], xr_sem.at[t]).wait()
+                pltpu.make_async_copy(cs_ref, tab.at[0, rows(t)], tr_sem.at[t]).wait()
+                tab_pair(t).start()
+
+            @pl.when(t > 0)
+            def _():
+                n_send(t - 1).start()
 
             norm_rows(gain, t)
-            if t > 0:
-                n_send(t - 1).start()
+            return 0
+
+        lax.fori_loop(0, 3, norm_chunk, 0)
 
         def qkv_tile(i, _):
             slot = lax.rem(i, 2)
@@ -207,6 +243,11 @@
                 def _():
                     for t in range(3):
                         n_send(t).wait_recv()
+
+                    @pl.when(l == 0)
+                    def _():
+                        for t in range(3):
+                            tab_pair(t).wait()
 
                     @pl.when(l > 0)
                     def _():
@@ -232,8 +273,11 @@
                     for j in range(8)])
                 piece = jnp.where(i < 4, 4 + 4 * lax.rem(i, 2) + 2 * (i // 2), 2 * (i - 4)) + s
                 plain = jnp.logical_and(lax.rem(i, 2) == 1, i < 4)
-                cos = jnp.where(plain, 1.0, tab_ref[0, s])
-                sin = jnp.where(plain, 0.0, tab_ref[1, s])
+                cs = tab[s]
+                sc = pltpu.roll(cs, 64, axis=1)
+                first = lax.broadcasted_iota(jnp.int32, (TOK, 128), 1) < 64
+                cos = jnp.where(plain, 1.0, jnp.where(first, cs, sc))
+                sin = jnp.where(plain, 0.0, jnp.where(first, -sc, cs))
                 for h in range(HG):
                     uh = u[:, h * 128:(h + 1) * 128]
                     pbuf[piece, :, h * 128:(h + 1) * 128] = (
@@ -299,7 +343,7 @@
                     total = jnp.sum(functools.reduce(jnp.add, es), axis=1, keepdims=True)
                     o = functools.reduce(jnp.add, [dot(e.astype(BF16), v) for e, (_, v, _) in zip(es, blocks)])
                     o = (o * (1.0 / total)).astype(BF16)
-                    obuf[core * 2 + g, rows(t), lanes] = o[:ROWS]
+                    pbuf[2 * g, rows(t), lanes] = o[:ROWS]
                     pbuf[2 * g + 1, rows(t), lanes] = o[ROWS:]
                 return 0
 
@@ -325,54 +369,58 @@
         for g in range(2):
             o_send(g).wait_recv()
 
+        def out_start(i):
+            @pl.when(i < 2 * n_out)
+            def _():
+                out_copy(l, i).start()
+
+            @pl.when(i >= 2 * n_out)
+            def _():
+                up_start(l, i - 2 * n_out)
+
         def out_tile(i, _):
-            out_copy(l, i).wait()
-
-            @pl.when(i < n_out - 1)
-            def _():
-                out_copy(l, i + 1).start()
-
-            @pl.when(i == n_out - 1)
-            def _():
-                up_copy(l, 0).start()
-
-            slot = t_slot(l, i)
-            u = functools.reduce(
-                jnp.add, [dot(obuf[j], ring[slot, j * TN:(j + 1) * TN, :]) for j in range(4)])
-            hbuf[:, cols(i)] = (hbuf[:, cols(i)].astype(F32) + u).astype(BF16)
+            out_copy(l, 2 * i).wait()
+            out_copy(l, 2 * i + 1).wait()
+
+            out_start(2 * i + 3)
+            out_start(2 * i + 4)
+            for j in range(2):
+                slot = t_slot(l, 2 * i + j)
+                mine = [dot(pbuf[2 * g], ring[slot, cols(2 * core + g), :]) for g in range(2)]
+                other = [dot(obuf[g], ring[slot, cols(2 - 2 * core + g), :]) for g in range(2)]
+                u = functools.reduce(jnp.add, mine + other)
+                c = half(2 * i + j)
+                hbuf[:, c] = (hbuf[:, c].astype(F32) + u).astype(BF16)
             return 0
 
         lax.fori_loop(0, n_out, out_tile, 0)
         for g in range(2):
             o_send(g).wait_send()
 
-        gain_m = gm_ref[l]
-        for t in range(3):
+        gain_m = gm_ref[pl.ds(l, 1), :]
+
+        def norm_mlp(t, _):
             norm_rows(gain_m, t)
+            return 0
+
+        lax.fori_loop(0, 3, norm_mlp, 0)
 
         def up_tile(i, _):
+            up_copy(l, 2 * i).wait()
+
             @pl.when(i < n_up - 1)
             def _():
-                up_copy(l, i).wait()
+                up_copy(l, 2 * i + 1).wait()
 
             @pl.when(i == n_up - 1)
             def _():
                 up_tail_copy(l).wait()
 
-            @pl.when(i < n_up - 2)
-            def _():
-                up_copy(l, i + 1).start()
-
-            @pl.when(i == n_up - 2)
-            def _():
-                up_tail_copy(l).start()
-
-            @pl.when(i == n_up - 1)
-            def _():
-                down_copy(l, 0, 0).start()
-
-            slot = t_slot(l, n_out + i)
-            pbuf[i] = gelu_tanh(dot(nbuf[0], ring[slot, 0:d_model, :])).astype(BF16)
+            up_start(l, 2 * i + 3)
+            up_start(l, 2 * i + 4)
+            for j in range(2):
+                slot = t_slot(l, 2 * n_out + 2 * i + j)
+                pbuf[i, :, j * TH:(j + 1) * TH] = gelu_tanh(dot(nbuf[0], ring[slot, 0:d_model, :])).astype(BF16)
             return 0
 
         lax.fori_loop(0, n_up, up_tile, 0)
@@ -380,9 +428,9 @@
         def y_send(c, t, n):
             dst, q = HOME[c][t]
             if dst == c:
-                return pltpu.make_async_copy(hbuf.at[rows(t), cols(n)], y_ref.at[q, :, cols(n)], yr_sem.at[q, n])
+                return pltpu.make_async_copy(hbuf.at[rows(t), half(n)], y_ref.at[q, :, half(n)], yr_sem.at[q, n])
             return pltpu.make_async_remote_copy(
-                src_ref=hbuf.at[rows(t), cols(n)], dst_ref=y_ref.at[q, :, cols(n)], send_sem=ys_sem.at[t, n],
+                src_ref=hbuf.at[rows(t), half(n)], dst_ref=y_ref.at[q, :, half(n)], send_sem=ys_sem.at[t, n],
                 recv_sem=yr_sem.at[q, n], device_id=on_chip(dst), device_id_type=MESH)
 
         def y_start(n):
@@ -392,40 +440,41 @@
                     for t in range(3):
                         y_send(c, t, n).start()
 
+        def down_start(n, kk, j):
+            @pl.when(n < n_out)
+            def _():
+                down_copy(l, n, kk, j).start()
+
+            @pl.when(jnp.logical_and(n >= n_out, l < n_layers - 1))
+            def _():
+                out_copy(l + 1, 2 * kk + j).start()
+
         def down_tile(n, _):
+            total = [None, None]
             for kk in range(3):
-                down_copy(l, n, kk).wait()
-                if kk < 2:
-                    down_copy(l, n, kk + 1).start()
-                else:
-                    @pl.when(n < n_out - 1)
-                    def _():
-                        down_copy(l, n + 1, 0).start()
-
-                    @pl.when(jnp.logical_and(n == n_out - 1, l < n_layers - 1))
-                    def _():
-                        out_copy(l + 1, 0).start()
-
+                for j in range(2):
+                    down_copy(l, n, kk, j).wait()
+                down_start(n + (kk + 1) // 3, (kk + 1) % 3, 1)
+                down_start(n + (kk + 2) // 3, (kk + 2) % 3, 0)
                 if kk == 0:
                     @pl.when(jnp.logical_and(n > 0, l == n_layers - 1))
                     def _():
-                        y_start(n - 1)
-
-                slot = t_slot(l, n_out + n_up + 3 * n + kk)
-                parts = []
-                lo = cuts[kk]
-                while lo < cuts[kk + 1]:
-                    hi = min((lo // TN + 1) * TN, cuts[kk + 1])
-                    parts.append(dot(pbuf[lo // TN, :, lo % TN:lo % TN + hi - lo],
-                                     ring[slot, lo - cuts[kk]:hi - cuts[kk], :]))
-                    lo = hi
-                u = functools.reduce(jnp.add, parts)
-                if kk == 0:
-                    acc[...] = u
-                elif kk == 1:
-                    acc[...] += u
-                else:
-                    hbuf[:, cols(n)] = (hbuf[:, cols(n)].astype(F32) + (acc[...] + u)).astype(BF16)
+                        y_start(2 * n - 2)
+                        y_start(2 * n - 1)
+
+                for j in range(2):
+                    slot = t_slot(l, 2 * n_out + up_tiles + 6 * n + 2 * kk + j)
+                    parts = [] if total[j] is None else [total[j]]
+                    lo = cuts[kk]
+                    while lo < cuts[kk + 1]:
+                        hi = min((lo // TN + 1) * TN, cuts[kk + 1])
+                        parts.append(dot(pbuf[lo // TN, :, lo % TN:lo % TN + hi - lo],
+                                         ring[slot, lo - cuts[kk]:hi - cuts[kk], :]))
+                        lo = hi
+                    total[j] = functools.reduce(jnp.add, parts)
+            for j in range(2):
+                c = half(2 * n + j)
+                hbuf[:, c] = (hbuf[:, c].astype(F32) + total[j]).astype(BF16)
             return 0
 
         lax.fori_loop(0, n_out, down_tile, 0)
@@ -440,27 +489,29 @@
                         pltpu.make_async_remote_copy(
                             src_ref=x_ref.at[q], dst_ref=hbuf.at[rows(slot)], send_sem=xs_sem.at[k],
                             recv_sem=xr_sem.at[slot], device_id=on_chip(dst), device_id_type=MESH).wait_send()
-            y_start(n_out - 1)
+                        tab_send(c, k, q).wait_send()
+            y_start(n_col - 2)
+            y_start(n_col - 1)
             for c in range(4):
                 @pl.when(chip == c)
                 def _(c=c):
-                    for n in range(n_out):
+                    for n in range(n_col):
                         for t in range(3):
                             if HOME[c][t][0] != c:
                                 y_send(c, t, n).wait_send()
-            for n in range(n_out):
+            for n in range(n_col):
                 for q in range(3):
-                    pltpu.make_async_copy(hbuf.at[rows(0), cols(n)], y_ref.at[q, :, cols(n)], yr_sem.at[q, n]).wait()
+                    pltpu.make_async_copy(hbuf.at[rows(0), half(n)], y_ref.at[q, :, half(n)], yr_sem.at[q, n]).wait()
 
         return 0
 
     lax.fori_loop(0, n_layers, layer, 0)
 
 
-def run_layers(x_loc, tab, g_attn, g_mlp, w_query, w_key, w_value, w_out, w_up, w_down):
+def run_layers(x_loc, cs_loc, g_attn, g_mlp, w_query, w_key, w_value, w_out, w_up, w_down):
     n_layers, d_model = g_attn.shape
     ff = w_up.shape[-1]
-    n_out = d_model // TN
+    n_col = d_model // TH
     k_units = ff // 256
     ring_rows = max(4 * TN, d_model, (k_units - 2 * (k_units // 3)) * 256)
     vmem = pl.BlockSpec(memory_space=pltpu.VMEM)
@@ -470,41 +521,34 @@
     return pl.pallas_call(
         functools.partial(layers_kernel, n_layers, d_model, ff),
         out_shape=jax.ShapeDtypeStruct(x_loc.shape, BF16),
-        in_specs=[hbm, vmem, vmem, vmem] + [hbm] * 6,
+        in_specs=[hbm, hbm, vmem, vmem] + [hbm] * 6,
         out_specs=hbm,
         scratch_shapes=[
             pltpu.VMEM((TOK, d_model), BF16),
             pltpu.VMEM((2, TOK, d_model), BF16),
             pltpu.VMEM((n_pieces, TOK, TN), BF16),
             pltpu.VMEM((4, 2, 2, ROWS, TN), BF16),
-            pltpu.VMEM((4, TOK, TN), BF16),
-            pltpu.VMEM((TOK, TN), F32),
+            pltpu.VMEM((2, TOK, TN), BF16),
+            pltpu.VMEM((2, TOK, 128), F32),
             pltpu.VMEM((2 * ROWS, 2 * ROWS), F32),
-            pltpu.VMEM((2, ring_rows, TN), BF16),
+            pltpu.VMEM((SLOTS, ring_rows, TH), BF16),
             pltpu.VMEM((2, d_model, HG, 128), BF16),
-            dma((2,)), dma((2,)), dma((2,)), dma((3,)), dma((3,)), dma((3,)),
-            dma((4, 2, 3)), dma((4, 2, 2)), dma((2,)), dma((2,)), dma((3, n_out)), dma((3, n_out)),
+            dma((SLOTS,)), dma((2,)), dma((2,)), dma((3,)), dma((2,)), dma((3,)), dma((3,)), dma((3,)),
+            dma((3,)), dma((3,)), dma((4, 2, 3)), dma((4, 2, 2)), dma((2,)), dma((2,)),
+            dma((3, n_col)), dma((3, n_col)),
             pltpu.SemaphoreType.REGULAR((2,)),
         ],
         compiler_params=pltpu.CompilerParams(
             collective_id=0, has_side_effects=True, vmem_limit_bytes=67043328),
         name="layers",
-    )(x_loc, tab, g_attn.reshape(n_layers, 1, d_model), g_mlp.reshape(n_layers, 1, d_model),
-      w_query, w_key, w_value, w_out.reshape(n_layers, -1, d_model), w_up, w_down)
-
-
-def rope_tables(pos_loc):
-    me = lax.axis_index("seq")
-    core, chip = me % 2, me // 2
-    pos_all = lax.all_gather(pos_loc, "seq")
-    home = jnp.array([[HOME[c][s][0] for s in range(3)] for c in range(4)], jnp.int32)
-    chunk = lax.dynamic_index_in_dim(home, chip, 0, keepdims=False)
-    side = jnp.stack([core, 1 - core])
-    pos = pos_all[(2 * chunk[None, :] + side[:, None])].reshape(2, TOK)
-    inv_freq = ROPE_BASE ** (-jnp.arange(64, dtype=F32) * (2.0 / 128))
-    angles = pos.astype(F32)[..., None] * inv_freq
-    cos, sin = jnp.cos(angles), jnp.sin(angles)
-    return jnp.stack([jnp.concatenate([cos, cos], -1), jnp.concatenate([-sin, sin], -1)])
+    )(x_loc, cs_loc, g_attn, g_mlp, w_query, w_key, w_value, w_out.reshape(n_layers, -1, d_model), w_up, w_down)
+
+
+def rope_table(pos_loc):
+    lane = lax.broadcasted_iota(jnp.int32, (1, 128), 1)
+    inv_freq = ROPE_BASE ** (-(lane % 64).astype(F32) * (2.0 / 128))
+    angles = pos_loc.astype(F32)[:, None] * inv_freq
+    return jnp.where(lane < 64, jnp.cos(angles), jnp.sin(angles))
 
 
 def solution(mesh):
@@ -512,7 +556,6 @@
     in_specs = (tok_spec, P(("data", "seq"))) + (P(),) * 8
 
     def device_fn(x_loc, pos_loc, w_query, w_key, w_value, w_out, w_up, w_down, g_attn, g_mlp):
-        tab = rope_tables(pos_loc)
-        return run_layers(x_loc, tab, g_attn, g_mlp, w_query, w_key, w_value, w_out, w_up, w_down)
+        return run_layers(x_loc, rope_table(pos_loc), g_attn, g_mlp, w_query, w_key, w_value, w_out, w_up, w_down)
 
     return jax.shard_map(device_fn, mesh=mesh, in_specs=in_specs, out_specs=tok_spec, check_vma=False)

time: 677 us -> 650 us (0.960)
  blocking collectives: 13.5 us -> 0 us
    all_gather x1 -> x0, blocking collectives: 13.5 us -> none  [rope_tables(): pos_all = lax.all_gather(pos_loc, 'seq')]
where the time goes in v2:
time: 650 us
  Pallas kernels  645 us (99%)
    pallas_call x1, Pallas kernels, run_layers(): pl.pallas_call(functools.partial(layers_kernel, n_layers, d_model, ff), o...  645 us

profile of v2, /device:TPU:0, one launch (start us, length us, event | category | flops | bytes accessed | tf_op | source)
XLA Modules:
  0.0 650.1 jit_solution(12827757490057151182)
XLA Ops:
  0.0 0.7 convert_element_type.11
  0.7 0.9 fusion.cs_ref
  1.6 644.5 %layers.1 = bf16[3,128,4096]{2,1,0:T(8,128)(2,1)} custom-call(bf16[3,128,4096]{2,1,0:T(8,128)(2,1)} %x_ref.1, f32[128,128]{1,0:T(8,128)} %fusion.cs_ref, f32[3,4096]{1,0:T(4,128)} %ga_ref.1, f32[3,4096]{1,0:T(4,128)} %gm_ref.1, bf16[3,4096,32,128]{3,2,1,0:T(8,128)(2,1)} %wq_ref.1, bf16[3,4096,32,128]{3,2,1,0:T(8,128)(2,1)} %wk_ref.1, ...), custom_call_target="tpu_custom_call" | custom-call | tf_op jit(solution)/shard_map/layers/pallas_call | solution.py:521
  646.2 3.9 copy.12
  (2 shorter events, 0.0 us)

commit v3 on v2

--- a/solution.py
+++ b/solution.py
@@ -26,7 +26,7 @@
     tuple(next((i, q) for i in range(4) for q in range(3) if ROUTE[i][q] == (c, s)) for s in range(3))
     for c in range(4)
 )
-KV_SENDS = (((0, 1, 0),), ((1, 2, 0), (2, 2, 1), (0, 0, 0)), ((0, 3, 0),), ())
+KV_SENDS = (((0, 1, 1),), ((1, 2, 2), (0, 1, 0)), ((0, 1, 3),), ())
 
 ROWS = 128
 TOK = 3 * ROWS
@@ -52,7 +52,7 @@
     x_ref, cs_ref, ga_ref, gm_ref, wq_ref, wk_ref, wv_ref, wo_ref, wu_ref, wd_ref,
     y_ref,
     hbuf, nbuf, pbuf, rbuf, obuf, tab, mask, ring, qring,
-    wsem, qsem, xs_sem, xr_sem, ts_sem, tr_sem, ps_sem, pr_sem, ns_sem, nr_sem, ks_sem, kr_sem, os_sem, or_sem,
+    wsem, qsem, xs_sem, xr_sem, ts_sem, tr_sem, ps_sem, pr_sem, ns_sem, nr_sem, ks_sem, kr_sem, kt_sem, ku_sem, os_sem, or_sem,
     ys_sem, yr_sem, cred,
 ):
     me = lax.axis_index("seq")
@@ -73,6 +73,14 @@
     def on_chip(c):
         return {"seq": 2 * c + core}
 
+    def by_core(order, send):
+        order = list(order)
+        if len(order) < 2:
+            send(order)
+        else:
+            pl.when(core == 0)(lambda: send(order))
+            pl.when(core == 1)(lambda: send(order[::-1]))
+
     def cols(i):
         return pl.ds(pl.multiple_of(i * TN, TN), TN)
 
@@ -154,12 +162,19 @@
     for c in range(4):
         @pl.when(chip == c)
         def _(c=c):
-            for k, q in enumerate(SEND_ORDER[c]):
-                dst, slot = ROUTE[c][q]
-                pltpu.make_async_remote_copy(
-                    src_ref=x_ref.at[q], dst_ref=hbuf.at[rows(slot)], send_sem=xs_sem.at[k],
-                    recv_sem=xr_sem.at[slot], device_id=on_chip(dst), device_id_type=MESH).start()
-                tab_send(c, k, q).start()
+            def send(order):
+                for q in order:
+                    k = SEND_ORDER[c].index(q)
+                    dst, slot = ROUTE[c][q]
+                    pltpu.make_async_remote_copy(
+                        src_ref=x_ref.at[q], dst_ref=hbuf.at[rows(slot)], send_sem=xs_sem.at[k],
+                        recv_sem=xr_sem.at[slot], device_id=on_chip(dst), device_id_type=MESH).start()
+                    tab_send(c, k, q).start()
+
+            if c == 2:
+                by_core(SEND_ORDER[c], send)
+            else:
+                send(SEND_ORDER[c])
             for q in range(3):
                 dst, slot = ROUTE[c][q]
                 if dst == c:
@@ -185,20 +200,36 @@
             src_ref=nbuf.at[0, rows(t)], dst_ref=nbuf.at[1, rows(t)], send_sem=ns_sem.at[t],
             recv_sem=nr_sem.at[t], device_id=partner, device_id_type=MESH)
 
-    def kv_send(i, s, k, slot, dst, rslot):
-        base = 4 + 4 * (i % 2) + 2 * (i // 2) if isinstance(i, int) else 4 + 4 * lax.rem(i, 2) + 2 * (i // 2)
+    def kv_send(i, s, k, slot, n, dst):
+        base = 4 + 4 * lax.rem(i, 2) + 2 * (i // 2)
         return pltpu.make_async_remote_copy(
-            src_ref=pbuf.at[base + s, rows(slot)], dst_ref=rbuf.at[i, rslot, s], send_sem=ks_sem.at[i, s, k],
-            recv_sem=kr_sem.at[i, rslot, s], device_id=on_chip(dst), device_id_type=MESH)
-
-    def kv_wait(i, s, rslot):
-        pltpu.make_async_remote_copy(
-            src_ref=pbuf.at[0, rows(0)], dst_ref=rbuf.at[i, rslot, s], send_sem=ks_sem.at[i, s, 0],
-            recv_sem=kr_sem.at[i, rslot, s], device_id=partner, device_id_type=MESH).wait_recv()
+            src_ref=pbuf.at[base + s, pl.ds(slot * ROWS, n * ROWS)],
+            dst_ref=rbuf.at[i, s, pl.ds(0, n * ROWS)], send_sem=ks_sem.at[i, s, k],
+            recv_sem=kr_sem.at[i, s], device_id=on_chip(dst), device_id_type=MESH)
+
+    def tail_copy(p, k, slot, n, dst):
+        lanes = pl.ds(pl.multiple_of(p * 256, 256), 256)
+        return pltpu.make_async_remote_copy(
+            src_ref=pbuf.at[11, pl.ds(slot * ROWS, n * ROWS), lanes],
+            dst_ref=rbuf.at[3, 1, pl.ds(0, n * ROWS), lanes], send_sem=kt_sem.at[k, p],
+            recv_sem=ku_sem.at[p], device_id=on_chip(dst), device_id_type=MESH)
+
+    def tail_wait(p, n):
+        tail_copy(p, 0, 0, n, 0).wait_recv()
+
+    def kv_wait(i, n, sides=(0, 1)):
+        for s in sides:
+            pltpu.make_async_remote_copy(
+                src_ref=pbuf.at[0, pl.ds(0, n * ROWS)], dst_ref=rbuf.at[i, s, pl.ds(0, n * ROWS)],
+                send_sem=ks_sem.at[i, s, 0], recv_sem=kr_sem.at[i, s], device_id=partner,
+                device_id_type=MESH).wait_recv()
+
+    def o_at(side, g):
+        return (2 * side + g) * TN
 
     def o_send(g):
         return pltpu.make_async_remote_copy(
-            src_ref=pbuf.at[2 * g + 1], dst_ref=obuf.at[g], send_sem=os_sem.at[g],
+            src_ref=nbuf.at[0, :, pl.ds(o_at(1, g), TN)], dst_ref=obuf.at[g], send_sem=os_sem.at[g],
             recv_sem=or_sem.at[g], device_id=partner, device_id_type=MESH)
 
     def layer(l, _):
@@ -254,7 +285,7 @@
                         for c in range(4):
                             @pl.when(chip == c)
                             def _(c=c):
-                                for k in sorted({1 if dst == 2 else 0 for _, dst, _ in KV_SENDS[c]}):
+                                for k in sorted({1 if dst == 2 else 0 for _, _, dst in KV_SENDS[c]}):
                                     pl.semaphore_wait(cred.at[k], 1)
 
                 @pl.when(jnp.logical_and(b >= 1, b <= 8))
@@ -264,8 +295,20 @@
                     for c in range(4):
                         @pl.when(chip == c)
                         def _(c=c):
-                            for k, (sl, dst, rs) in enumerate(KV_SENDS[c]):
-                                kv_send(pi, ps, k, sl, dst, rs).start()
+                            def send(order):
+                                for k in order:
+                                    sl, n, dst = KV_SENDS[c][k]
+
+                                    @pl.when(b < 8)
+                                    def _(k=k, sl=sl, n=n, dst=dst):
+                                        kv_send(pi, ps, k, sl, n, dst).start()
+
+                                    @pl.when(b == 8)
+                                    def _(k=k, sl=sl, n=n, dst=dst):
+                                        for p in range(4):
+                                            tail_copy(p, k, sl, n, dst).start()
+
+                            by_core(range(len(KV_SENDS[c])), send)
 
                 kq = d_model // 8
                 u = functools.reduce(jnp.add, [
@@ -283,10 +326,6 @@
                     pbuf[piece, :, h * 128:(h + 1) * 128] = (
                         uh * cos + pltpu.roll(uh, 64, axis=1) * sin).astype(BF16)
 
-                @pl.when(jnp.logical_and(i < 4, chip != 2))
-                def _():
-                    rbuf[jnp.minimum(i, 3), 1, s] = pbuf[piece, 0:ROWS, :]
-
                 return 0
 
             lax.fori_loop(0, 2, side, 0)
@@ -296,69 +335,109 @@
         for t in range(3):
             n_send(t).wait_send()
 
-        bias0 = jnp.where(lax.rem(chip, 2) == 1, 0.0, NEG)
-        bias1 = jnp.where(chip == 1, NEG, 0.0)
         c2 = 128 ** -0.5 * LOG2E
 
-        def group(g, _):
-            for j in range(2):
-                for s in range(2):
-                    kv_wait(2 * g + j, s, 0)
-
-            @pl.when(chip == 2)
-            def _():
-                for j in range(2):
-                    for s in range(2):
-                        kv_wait(2 * g + j, s, 1)
-
-            @pl.when(g == 1)
-            def _():
-                o_send(0).start()
-
-            def head(h, _):
-                lanes = pl.ds(pl.multiple_of(h * 128, 128), 128)
-
-                def local(base, t):
-                    r = rows(t)
-                    return jnp.concatenate([pbuf[base + 2 * g, r, lanes], pbuf[base + 2 * g + 1, r, lanes]], axis=0)
-
-                def remote(j, rs):
-                    return jnp.concatenate([rbuf[2 * g + j, rs, 0, :, lanes], rbuf[2 * g + j, rs, 1, :, lanes]], axis=0)
-
-                for t in range(3):
-                    q = local(0, t)
-                    blocks = [(remote(0, 0), remote(1, 0), bias0 if t == 0 else bias1)]
-                    if t > 0:
-                        blocks.append((remote(0, 1), remote(1, 1), bias1))
-                    if t == 2:
-                        blocks.append((local(4, 1), local(8, 1), None))
-                    blocks.append((local(4, t), local(8, t), mask[...]))
-                    xs = []
-                    for k, _, b in blocks:
-                        sc = lax.dot_general(q, k, (((1,), (1,)), ((), ())), preferred_element_type=F32) * c2
-                        xs.append(sc if b is None else sc + b)
-                    top = functools.reduce(jnp.maximum, xs)
-                    top = jnp.max(top, axis=1, keepdims=True)
-                    es = [jnp.exp2(v - top) for v in xs]
-                    total = jnp.sum(functools.reduce(jnp.add, es), axis=1, keepdims=True)
-                    o = functools.reduce(jnp.add, [dot(e.astype(BF16), v) for e, (_, v, _) in zip(es, blocks)])
-                    o = (o * (1.0 / total)).astype(BF16)
-                    pbuf[2 * g, rows(t), lanes] = o[:ROWS]
-                    pbuf[2 * g + 1, rows(t), lanes] = o[ROWS:]
-                return 0
-
-            lax.fori_loop(0, HG, head, 0)
-            return 0
-
-        lax.fori_loop(0, 2, group, 0)
+        def attend(g, h, t, others):
+            lanes = pl.ds(pl.multiple_of(h * 128, 128), 128)
+
+            def local(base, u):
+                return [pbuf[base + 2 * g + s, rows(u), lanes] for s in range(2)]
+
+            def block(j, u):
+                if isinstance(u, str):
+                    return jnp.concatenate([rbuf[2 * g + j, s, rows(int(u[1])), lanes] for s in range(2)], axis=0)
+                return jnp.concatenate(local(4 + 4 * j, u), axis=0)
+
+            def score(q, k):
+                return lax.dot_general(q, k, (((1,), (1,)), ((), ())), preferred_element_type=F32) * c2
+
+            q = jnp.concatenate(local(0, t), axis=0)
+            slots = list(others) + [t]
+            xs = [lax.dot_general(q, block(0, u), (((1,), (1,)), ((), ())), preferred_element_type=F32) * c2 for u in slots]
+            xs[-1] = xs[-1] + mask[...]
+            top = jnp.max(functools.reduce(jnp.maximum, xs), axis=1, keepdims=True)
+            es = [jnp.exp2(x - top) for x in xs]
+            total = jnp.sum(functools.reduce(jnp.add, es), axis=1, keepdims=True)
+            o = functools.reduce(jnp.add, [dot(e.astype(BF16), block(1, u)) for e, u in zip(es, slots)])
+            o = (o * (1.0 / total)).astype(BF16)
+            for s in range(2):
+                nbuf[0, rows(t), pl.ds(pl.multiple_of(o_at(s, g) + h * 128, 128), 128)] = o[s * ROWS:(s + 1) * ROWS]
+
+        def group_wait(g, n):
+            kv_wait(2 * g, n)
+            kv_wait(2 * g + 1, n, (0,))
+
+            @pl.when(g == 0)
+            def _():
+                kv_wait(1, n, (1,))
+
+        def heads(g, work, n=None):
+            def step(h, c):
+                if n is not None:
+                    @pl.when(jnp.logical_and(g == 1, lax.rem(h, 2) == 0))
+                    def _():
+                        tail_wait(h // 2, n)
+
+                for t, others in work[::-1]:
+                    attend(g, h, t, others)
+                return c
+
+            lax.fori_loop(0, HG, step, 0)
+
+        def groups(n, work):
+            def step(g, c):
+                group_wait(g, n)
+
+                @pl.when(g == 1)
+                def _():
+                    o_send(0).start()
+
+                heads(g, work, n)
+                return c
+
+            lax.fori_loop(0, 2, step, 0)
+
+        @pl.when(chip == 0)
+        def _():
+            groups(1, ((0, ()), (1, ("r0", 0)), (2, ("r0", 0, 1))))
+
+        @pl.when(chip == 1)
+        def _():
+            def first_step(g, c):
+                heads(g, ((1, ()), (2, (1,))))
+                return c
+
+            lax.fori_loop(0, 2, first_step, 0)
+
+            def last_step(g, c):
+                group_wait(g, 1)
+
+                @pl.when(g == 1)
+                def _():
+                    o_send(0).start()
+
+                heads(g, ((0, ("r0",)),), 1)
+                return c
+
+            lax.fori_loop(0, 2, last_step, 0)
+
+        @pl.when(chip == 2)
+        def _():
+            groups(2, ((0, ()), (1, ("r0", "r1")), (2, ("r0", "r1", 1))))
+
+        @pl.when(chip == 3)
+        def _():
+            groups(1, ((0, ("r0",)), (1, ("r0", 0)), (2, ("r0", 0, 1))))
 
         for c in range(4):
             @pl.when(chip == c)
             def _(c=c):
-                for i in range(4):
-                    for s in range(2):
-                        for k, (sl, dst, rs) in enumerate(KV_SENDS[c]):
-                            kv_send(i, s, k, sl, dst, rs).wait_send()
+                for k, (sl, n, dst) in enumerate(KV_SENDS[c]):
+                    for i in range(4):
+                        for s in range(2 if i < 3 else 1):
+                            kv_send(i, s, k, sl, n, dst).wait_send()
+                    for p in range(4):
+                        tail_copy(p, k, sl, n, dst).wait_send()
 
                 @pl.when(l < n_layers - 1)
                 def _():
@@ -366,8 +445,6 @@
                     pl.semaphore_signal(cred.at[k], inc=1, device_id=on_chip(src), device_id_type=MESH)
 
         o_send(1).start()
-        for g in range(2):
-            o_send(g).wait_recv()
 
         def out_start(i):
             @pl.when(i < 2 * n_out)
@@ -384,13 +461,19 @@
 
             out_start(2 * i + 3)
             out_start(2 * i + 4)
-            for j in range(2):
-                slot = t_slot(l, 2 * i + j)
-                mine = [dot(pbuf[2 * g], ring[slot, cols(2 * core + g), :]) for g in range(2)]
+            slots = [t_slot(l, 2 * i + j) for j in range(2)]
+            us = [functools.reduce(jnp.add, [dot(nbuf[0, :, o_at(0, g):o_at(0, g) + TN], ring[slot, cols(2 * core + g), :]) for g in range(2)])
+                  for slot in slots]
+
+            @pl.when(i == 0)
+            def _():
+                for g in range(2):
+                    o_send(g).wait_recv()
+
+            for j, slot in enumerate(slots):
                 other = [dot(obuf[g], ring[slot, cols(2 - 2 * core + g), :]) for g in range(2)]
-                u = functools.reduce(jnp.add, mine + other)
                 c = half(2 * i + j)
-                hbuf[:, c] = (hbuf[:, c].astype(F32) + u).astype(BF16)
+                hbuf[:, c] = (hbuf[:, c].astype(F32) + (us[j] + functools.reduce(jnp.add, other))).astype(BF16)
             return 0
 
         lax.fori_loop(0, n_out, out_tile, 0)
@@ -437,8 +520,15 @@
             for c in range(4):
                 @pl.when(chip == c)
                 def _(c=c):
-                    for t in range(3):
-                        y_send(c, t, n).start()
+                    def send(order):
+                        for t in order:
+                            y_send(c, t, n).start()
+
+                    if c == 2:
+                        by_core((0, 2), send)
+                        send((1,))
+                    else:
+                        send(range(3))
 
         def down_start(n, kk, j):
             @pl.when(n < n_out)
@@ -527,14 +617,14 @@
             pltpu.VMEM((TOK, d_model), BF16),
             pltpu.VMEM((2, TOK, d_model), BF16),
             pltpu.VMEM((n_pieces, TOK, TN), BF16),
-            pltpu.VMEM((4, 2, 2, ROWS, TN), BF16),
+            pltpu.VMEM((4, 2, 2 * ROWS, TN), BF16),
             pltpu.VMEM((2, TOK, TN), BF16),
             pltpu.VMEM((2, TOK, 128), F32),
             pltpu.VMEM((2 * ROWS, 2 * ROWS), F32),
             pltpu.VMEM((SLOTS, ring_rows, TH), BF16),
             pltpu.VMEM((2, d_model, HG, 128), BF16),
             dma((SLOTS,)), dma((2,)), dma((2,)), dma((3,)), dma((2,)), dma((3,)), dma((3,)), dma((3,)),
-            dma((3,)), dma((3,)), dma((4, 2, 3)), dma((4, 2, 2)), dma((2,)), dma((2,)),
+            dma((3,)), dma((3,)), dma((4, 2, 2)), dma((4, 2)), dma((2, 4)), dma((4,)), dma((2,)), dma((2,)),
             dma((3, n_col)), dma((3, n_col)),
             pltpu.SemaphoreType.REGULAR((2,)),
         ],

time: 650 us -> 644 us (level)
  Pallas kernels: 645 us -> 638 us
    pallas_call x1, Pallas kernels: 645 us -> 638 us  [run_layers(): pl.pallas_call(functools.partial(layers_kernel, n_layers, d_model, ff), o...]
where the time goes in v3:
time: 644 us
  Pallas kernels  638 us (99%)
    pallas_call x1, Pallas kernels, run_layers(): pl.pallas_call(functools.partial(layers_kernel, n_layers, d_model, ff), o...  638 us

profile of v3, /device:TPU:0, one launch (start us, length us, event | category | flops | bytes accessed | tf_op | source)
XLA Modules:
  0.0 643.5 jit_solution(9798645728092018157)
XLA Ops:
  0.0 0.7 convert_element_type.11
  0.7 0.9 fusion.cs_ref
  1.6 638.0 %layers.1 = bf16[3,128,4096]{2,1,0:T(8,128)(2,1)} custom-call(bf16[3,128,4096]{2,1,0:T(8,128)(2,1)} %x_ref.1, f32[128,128]{1,0:T(8,128)} %fusion.cs_ref, f32[3,4096]{1,0:T(4,128)} %ga_ref.1, f32[3,4096]{1,0:T(4,128)} %gm_ref.1, bf16[3,4096,32,128]{3,2,1,0:T(8,128)(2,1)} %wq_ref.1, bf16[3,4096,32,128]{3,2,1,0:T(8,128)(2,1)} %wk_ref.1, ...), custom_call_target="tpu_custom_call" | custom-call | tf_op jit(solution)/shard_map/layers/pallas_call | solution.py:611
  639.6 3.9 copy.12
  (2 shorter events, 0.0 us)
